TPU v7x, 64 devices: a 2x2x8 block of a 4x4x8 slice. The times are simulated.
64 devices in a mesh: replica: 4 (over x, y), dp: 16 (over z, core).
Axes of the slice: x: 2, y: 2, z: 8, core: 2. Of those that a mesh axis runs over, the one named last changes fastest.
The devices are a block of a 4x4x8 slice.
Arguments:
- x: bfloat16 [1024, 448], P(('replica', 'dp')), parts along dimension 0
- lengths: int32 [1024], P(('replica', 'dp')), parts along dimension 0
- cache: bfloat16 [2, 1024, 512, 576], P(None, ('replica', 'dp')), parts along dimension 1
- w_q: bfloat16 [2, 448, 2304], replicated
- w_o: bfloat16 [2, 2048, 448], replicated
- expert_ids: int32 [2, 1024, 8], P(None, ('replica', 'dp')), parts along dimension 1
- slots: int32 [2, 1024, 8], P(None, ('replica', 'dp')), parts along dimension 1
- route_w: float32 [2, 1024, 8], P(None, ('replica', 'dp')), parts along dimension 1
- w1_exp: bfloat16 [2, 384, 448, 128], P(None, 'dp')
- w3_exp: bfloat16 [2, 384, 448, 128], P(None, 'dp')
- w2_exp: bfloat16 [2, 384, 128, 448], P(None, 'dp')
- w1_sh: bfloat16 [2, 448, 128], P(None, None, 'dp')
- w3_sh: bfloat16 [2, 448, 128], P(None, None, 'dp')
- w2_sh: bfloat16 [2, 128, 448], P(None, 'dp')
Outputs:
- output: bfloat16 [1024, 448], P(('replica', 'dp')), parts along dimension 0
There are 4 independent parts. A program takes and returns all parts, laid end to end along the dimension named above; an argument that names none is the same for every part.
All inputs are finite; a program needn't handle non-finite values.
Results may differ from a plain program's by a relative error of at most 0.02.
Values are sent between devices in bfloat16 or wider.
A program may use at most 768 MiB of HBM per device.

v0:
```python
import jax
import jax.numpy as jnp
from jax import lax
from jax.sharding import PartitionSpec as P

NORM_EPS = 1e-6
ATT_SCALE = 1.0 / (192.0 ** 0.5)
LATENT = 512


def rms_norm(values):
    vals32 = values.astype(jnp.float32)
    return vals32 * lax.rsqrt(jnp.mean(vals32 * vals32, axis=-1, keepdims=True) + NORM_EPS)


def gated_hidden(tok_in, w_up, w_gate):
    gate_in = jnp.dot(tok_in, w_gate, preferred_element_type=jnp.float32)
    up_in = jnp.dot(tok_in, w_up, preferred_element_type=jnp.float32)
    return (jax.nn.silu(gate_in) * up_in).astype(jnp.bfloat16)


def local_attention(resid, lengths, cache_l, w_q_l, w_o_l):
    tok_count = resid.shape[0]
    seq_len, kv_dim = cache_l.shape[1], cache_l.shape[2]
    num_heads = w_q_l.shape[1] // kv_dim
    normed = rms_norm(resid).astype(jnp.bfloat16)
    queries = jnp.dot(normed, w_q_l, preferred_element_type=jnp.float32).astype(jnp.bfloat16)
    queries = queries.reshape(tok_count, num_heads, kv_dim)
    scores = jnp.einsum('bhc,btc->bht', queries, cache_l, preferred_element_type=jnp.float32) * ATT_SCALE
    valid = jnp.arange(seq_len)[None, None, :] < lengths[:, None, None]
    probs = jax.nn.softmax(jnp.where(valid, scores, -jnp.inf), axis=-1).astype(jnp.bfloat16)
    attn = jnp.einsum('bht,btc->bhc', probs, cache_l[:, :, :LATENT], preferred_element_type=jnp.float32)
    attn = attn.astype(jnp.bfloat16).reshape(tok_count, num_heads * LATENT)
    return (resid.astype(jnp.float32) + jnp.dot(attn, w_o_l, preferred_element_type=jnp.float32)).astype(jnp.bfloat16)


def route_select(ids_l, slot_l, experts, capacity):
    buf_rows = jnp.where(slot_l >= 0, ids_l * capacity + slot_l, -1)
    return (buf_rows[:, :, None] == jnp.arange(experts * capacity)).astype(jnp.bfloat16)


def solution(mesh):
    group = mesh.shape['dp']
    tok_axes = ('replica', 'dp')
    in_specs = (
        P(tok_axes, None), P(tok_axes), P(None, tok_axes, None, None),
        P(None, None, None), P(None, None, None),
        P(None, tok_axes, None), P(None, tok_axes, None), P(None, tok_axes, None),
        P(None, 'dp', None, None), P(None, 'dp', None, None), P(None, 'dp', None, None),
        P(None, None, 'dp'), P(None, None, 'dp'), P(None, 'dp', None),
    )

    def device_step(x, lengths, cache, w_q, w_o, expert_ids, slots, route_w, w1_exp, w3_exp, w2_exp, w1_sh, w3_sh, w2_sh):
        batch_dev, d_model = x.shape
        local_experts = w1_exp.shape[1]
        experts = local_experts * group
        top_k = expert_ids.shape[2]
        capacity = max(1, (2 * batch_dev * top_k) // experts)
        resid = x
        for layer_idx in range(cache.shape[0]):
            resid = local_attention(resid, lengths, cache[layer_idx], w_q[layer_idx], w_o[layer_idx])
            ffn_in = rms_norm(resid).astype(jnp.bfloat16)
            gathered = lax.all_gather(ffn_in, 'dp', axis=0, tiled=True)
            shared_h = gated_hidden(gathered, w1_sh[layer_idx], w3_sh[layer_idx])
            shared_part = jnp.dot(shared_h, w2_sh[layer_idx], preferred_element_type=jnp.float32)
            shared_out = lax.psum_scatter(shared_part, 'dp', scatter_dimension=0, tiled=True)
            select = route_select(expert_ids[layer_idx], slots[layer_idx], experts, capacity)
            dispatch = jnp.sum(select, axis=1)
            send_buf = jnp.einsum('br,bd->rd', dispatch, ffn_in, preferred_element_type=jnp.float32).astype(jnp.bfloat16)
            send_buf = send_buf.reshape(group, local_experts, capacity, d_model)
            recv_buf = lax.all_to_all(send_buf, 'dp', 0, 0, tiled=True)
            gate_in = jnp.einsum('sncd,ndf->nscf', recv_buf, w3_exp[layer_idx], preferred_element_type=jnp.float32)
            up_in = jnp.einsum('sncd,ndf->nscf', recv_buf, w1_exp[layer_idx], preferred_element_type=jnp.float32)
            hidden = (jax.nn.silu(gate_in) * up_in).astype(jnp.bfloat16)
            expert_out = jnp.einsum('nscf,nfd->sncd', hidden, w2_exp[layer_idx], preferred_element_type=jnp.float32).astype(jnp.bfloat16)
            returned = lax.all_to_all(expert_out, 'dp', 0, 0, tiled=True)
            returned = returned.reshape(experts * capacity, d_model)
            picked = jnp.einsum('cls,se->cle', select, returned, preferred_element_type=jnp.float32)
            routed = jnp.sum(route_w[layer_idx][:, :, None] * picked, axis=1)
            resid = (resid.astype(jnp.float32) + routed + shared_out).astype(jnp.bfloat16)
        return resid

    return jax.shard_map(device_step, mesh=mesh, in_specs=in_specs, out_specs=P(tok_axes, None), check_vma=False)
```

profile of v0, /device:TPU:21, one launch (start us, length us, event | category | flops | bytes accessed | tf_op | source)
XLA Modules:
  0.0 237.1 jit_solution(3527744597225843789)
XLA Ops:
  8.1 2.0 convolution_convert_fusion.1
  10.3 14.2 %slice_bitcast_fusion.1 = (bf16[16,512,576]{1,2,0:T(8,128)(2,1)}, bf16[16,512,576]{1,2,0:T(8,128)(2,1)}) fusion(bf16[2,16,512,576]{2,3,1,0:T(8,128)(2,1)} %param.16), kind=kLoop, calls=%fused_computation.3 | loop fusion | bytes 37748736 | tf_op jit(solution)/shard_map/squeeze | solution.py:61
  24.5 5.2 %fusion.172 = (f32[16,4]{1,0:T(8,128)S(1)}, f32[16,4,512]{2,1,0:T(4,128)S(1)}) fusion(bf16[16,4,576]{2,1,0:T(4,128)(2,1)S(1)} %reshape.155, pred[16,512]{1,0:T(8,128)(4,1)S(1)} %iota_compare_fusion.4, bf16[2,16,512,576]{2,3,1,0:T(8,128)(2,1)} %param.16), kind=kOutput, calls=%fused_computation.161 | convolution fusion | flops 37880320 | bytes 9650432 | tf_op jit(solution)/shard_map/sub | solution.py:31
  29.7 5.8 %fusion.66 = bf16[16,4,512]{2,1,0:T(4,128)(2,1)S(1)} fusion(bf16[16,512,576]{1,2,0:T(8,128)(2,1)} %get-tuple-element.7, f32[16,4,512]{2,1,0:T(4,128)S(1)} %get-tuple-element.14, f32[16,4]{1,0:T(8,128)S(1)} %get-tuple-element.13), kind=kOutput, calls=%fused_computation.60 | convolution fusion | flops 33652736 | bytes 8585472 | tf_op jit(solution)/shard_map/bht,btc->bhc/dot_general | solution.py:32
  37.9 10.7 %all-to-all-start = ((bf16[16,24,1,448]{3,1,2,0:T(8,128)(2,1)}), bf16[16,24,1,448]{3,1,2,0:T(8,128)(2,1)S(1)}, u32[]{:S(2)}, u32[]{:S(2)}) async-start(bf16[16,24,1,448]{3,1,2,0:T(8,128)(2,1)} %bitcast.6), calls=%async_computation | async-start | bytes 786432 | tf_op jit(solution)/shard_map/all_to_all | solution.py:71
  48.7 22.9 %all_gather.6 = bf16[256,448]{1,0:T(8,128)(2,1)S(1)} all-gather(bf16[16,448]{1,0:T(8,128)(2,1)S(1)} %multiply_convert_fusion.1), channel_id=1, replica_groups=mesh['replica'=4,'dp'=16] {'dp'}, dimensions={0}, use_global_device_ids=true | all-gather | bytes 243712 | tf_op jit(solution)/shard_map/all_gather | solution.py:63
  71.7 1.4 fusion.93
  73.2 2.4 %fusion.16 = f32[24,16,128]{2,1,0:T(8,128)S(1)} fusion(bf16[2,24,448,128]{3,2,1,0:T(8,128)(2,1)} %param.23, bf16[16,24,1,448]{3,1,2,0:T(8,128)(2,1)S(1)} %all-to-all-done), kind=kOutput, calls=%fused_computation.20 | convolution fusion | flops 44040192 | bytes 3293184 | tf_op jit(solution)/shard_map/sncd,ndf->nscf/dot_general | solution.py:72
  75.6 4.3 %fusion.43 = bf16[16,24,1,448]{3,0,1,2:T(8,128)(2,1)S(1)} fusion(bf16[2,24,128,448]{2,3,1,0:T(8,128)(2,1)} %param.24, bf16[2,24,448,128]{3,2,1,0:T(8,128)(2,1)} %param.22, bf16[16,24,1,448]{3,1,2,0:T(8,128)(2,1)S(1)} %all-to-all-done, f32[24,16,128]{2,1,0:T(8,128)S(1)} %fusion.16), kind=kOutput, calls=%fused_computation.43 | convolution fusion | flops 88547328 | bytes 6389760 | tf_op jit(solution)/shard_map/nscf,nfd->sncd/dot_general | solution.py:75
  80.9 6.4 %all-to-all-start.1 = ((bf16[16,24,1,448]{3,1,2,0:T(8,128)(2,1)}), bf16[16,24,1,448]{3,1,2,0:T(8,128)(2,1)S(1)}, u32[]{:S(2)}, u32[]{:S(2)}) async-start(bf16[16,24,1,448]{3,1,2,0:T(8,128)(2,1)} %copy.43), calls=%async_computation.1 | async-start | bytes 786432 | tf_op jit(solution)/shard_map/all_to_all | solution.py:76
  87.6 14.4 %all-to-all-done.1 = bf16[16,24,1,448]{3,1,2,0:T(8,128)(2,1)S(1)} async-done(((bf16[16,24,1,448]{3,1,2,0:T(8,128)(2,1)}), bf16[16,24,1,448]{3,1,2,0:T(8,128)(2,1)S(1)}, u32[]{:S(2)}, u32[]{:S(2)}) %all-to-all-start.1) | async-done | bytes 344096 | tf_op jit(solution)/shard_map/all_to_all | solution.py:76
  102.3 23.8 %reduce-scatter.3.cloned.1.call-done = f32[16,448]{1,0:T(8,128)} async-done(((f32[256,448]{1,0:T(8,128)}), f32[16,448]{1,0:T(8,128)}) %reduce-scatter.3.cloned.1.call-update) | async-done | bytes 28688 | tf_op jit(solution)/shard_map/reduce_scatter | solution.py:66
  127.0 2.0 convolution_convert_fusion
  129.1 5.2 %fusion.173 = (f32[16,4]{1,0:T(8,128)S(1)}, f32[16,4,512]{2,1,0:T(4,128)S(1)}) fusion(bf16[16,4,576]{2,1,0:T(4,128)(2,1)S(1)} %reshape.160, pred[16,512]{1,0:T(8,128)(4,1)S(1)} %iota_compare_fusion.4, bf16[2,16,512,576]{2,3,1,0:T(8,128)(2,1)} %param.16), kind=kOutput, calls=%fused_computation.162 | convolution fusion | flops 37880320 | bytes 9650432 | tf_op jit(solution)/shard_map/sub | solution.py:31
  134.3 5.8 %fusion.69 = bf16[16,4,512]{2,1,0:T(4,128)(2,1)S(1)} fusion(bf16[16,512,576]{1,2,0:T(8,128)(2,1)} %get-tuple-element.8, f32[16,4,512]{2,1,0:T(4,128)S(1)} %get-tuple-element.18, f32[16,4]{1,0:T(8,128)S(1)} %get-tuple-element.17), kind=kOutput, calls=%fused_computation.61 | convolution fusion | flops 33652736 | bytes 8585472 | tf_op jit(solution)/shard_map/bht,btc->bhc/dot_general | solution.py:32
  142.2 8.8 %all-to-all-start.2 = ((bf16[16,24,1,448]{3,1,2,0:T(8,128)(2,1)}), bf16[16,24,1,448]{3,1,2,0:T(8,128)(2,1)S(1)}, u32[]{:S(2)}, u32[]{:S(2)}) async-start(bf16[16,24,1,448]{3,1,2,0:T(8,128)(2,1)} %bitcast.25), calls=%async_computation.3 | async-start | bytes 786432 | tf_op jit(solution)/shard_map/all_to_all | solution.py:71
  151.1 22.9 %all_gather.7 = bf16[256,448]{1,0:T(8,128)(2,1)S(1)} all-gather(bf16[16,448]{1,0:T(8,128)(2,1)S(1)} %multiply_convert_fusion), channel_id=1, replica_groups=mesh['replica'=4,'dp'=16] {'dp'}, dimensions={0}, use_global_device_ids=true | all-gather | bytes 243712 | tf_op jit(solution)/shard_map/all_gather | solution.py:63
  174.1 1.4 fusion.92
  175.6 2.4 %fusion.10 = f32[24,16,128]{2,1,0:T(8,128)S(1)} fusion(bf16[2,24,448,128]{3,2,1,0:T(8,128)(2,1)} %param.23, bf16[16,24,1,448]{3,1,2,0:T(8,128)(2,1)S(1)} %all-to-all-done.2), kind=kOutput, calls=%fused_computation.14 | convolution fusion | flops 44040192 | bytes 3293184 | tf_op jit(solution)/shard_map/sncd,ndf->nscf/dot_general | solution.py:72
  178.0 4.3 %fusion.40 = bf16[16,24,1,448]{3,0,1,2:T(8,128)(2,1)S(1)} fusion(bf16[2,24,128,448]{2,3,1,0:T(8,128)(2,1)} %param.24, bf16[2,24,448,128]{3,2,1,0:T(8,128)(2,1)} %param.22, bf16[16,24,1,448]{3,1,2,0:T(8,128)(2,1)S(1)} %all-to-all-done.2, f32[24,16,128]{2,1,0:T(8,128)S(1)} %fusion.10), kind=kOutput, calls=%fused_computation.42 | convolution fusion | flops 88547328 | bytes 6389760 | tf_op jit(solution)/shard_map/nscf,nfd->sncd/dot_general | solution.py:75
  183.3 6.4 %all-to-all-start.3 = ((bf16[16,24,1,448]{3,1,2,0:T(8,128)(2,1)}), bf16[16,24,1,448]{3,1,2,0:T(8,128)(2,1)S(1)}, u32[]{:S(2)}, u32[]{:S(2)}) async-start(bf16[16,24,1,448]{3,1,2,0:T(8,128)(2,1)} %copy.51), calls=%async_computation.4 | async-start | bytes 786432 | tf_op jit(solution)/shard_map/all_to_all | solution.py:76
  189.7 14.5 %all-to-all-done.3 = bf16[16,24,1,448]{3,1,2,0:T(8,128)(2,1)S(1)} async-done(((bf16[16,24,1,448]{3,1,2,0:T(8,128)(2,1)}), bf16[16,24,1,448]{3,1,2,0:T(8,128)(2,1)S(1)}, u32[]{:S(2)}, u32[]{:S(2)}) %all-to-all-start.3) | async-done | bytes 344096 | tf_op jit(solution)/shard_map/all_to_all | solution.py:76
  204.6 24.3 %reduce-scatter.5.cloned.1.call-done = f32[16,448]{1,0:T(8,128)} async-done(((f32[256,448]{1,0:T(8,128)}), f32[16,448]{1,0:T(8,128)}) %reduce-scatter.5.cloned.1.call-update) | async-done | bytes 28688 | tf_op jit(solution)/shard_map/reduce_scatter | solution.py:66
  228.9 1.4 add_convert_fusion
  (57 shorter events, 10.6 us)
Async XLA Ops:
  29.7 5.9 %copy-start = (bf16[2,2048,448]{1,2,0:T(8,128)(2,1)S(1)}, bf16[2,2048,448]{1,2,0:T(8,128)(2,1)}, u32[]{:S(2)}) copy-start(bf16[2,2048,448]{1,2,0:T(8,128)(2,1)} %param.18) | copy-start | bytes 11010052
  29.7 5.9 %copy-start.2 = (bf16[16,448]{1,0:T(8,128)(2,1)S(1)}, bf16[16,448]{1,0:T(8,128)(2,1)}, u32[]{:S(2)}) copy-start(bf16[16,448]{1,0:T(8,128)(2,1)} %param.14) | copy-start | bytes 43012
  29.7 6.6 %copy-start.6 = (s32[2,16,8]{1,2,0:T(8,128)S(1)}, s32[2,16,8]{1,2,0:T(8,128)}, u32[]{:S(2)}) copy-start(s32[2,16,8]{1,2,0:T(8,128)} %param.19) | copy-start | bytes 3076
  29.7 6.6 %copy-start.7 = (s32[2,16,8]{1,2,0:T(8,128)S(1)}, s32[2,16,8]{1,2,0:T(8,128)}, u32[]{:S(2)}) copy-start(s32[2,16,8]{1,2,0:T(8,128)} %param.20) | copy-start | bytes 3076
  29.7 41.9 %copy-start.5 = (bf16[2,448,8]{1,2,0:T(8,128)(2,1)S(1)}, bf16[2,448,8]{1,2,0:T(8,128)(2,1)}, u32[]{:S(2)}) copy-start(bf16[2,448,8]{1,2,0:T(8,128)(2,1)} %param.26) | copy-start | bytes 43012
  29.7 42.0 %copy-start.3 = (bf16[2,8,448]{2,1,0:T(8,128)(2,1)S(1)}, bf16[2,8,448]{2,1,0:T(8,128)(2,1)}, u32[]{:S(2)}) copy-start(bf16[2,8,448]{2,1,0:T(8,128)(2,1)} %param.27) | copy-start | bytes 43012
  29.7 42.0 %copy-start.4 = (bf16[2,448,8]{1,2,0:T(8,128)(2,1)S(1)}, bf16[2,448,8]{1,2,0:T(8,128)(2,1)}, u32[]{:S(2)}) copy-start(bf16[2,448,8]{1,2,0:T(8,128)(2,1)} %param.25) | copy-start | bytes 43012
  37.9 35.3 %all-to-all-start = ((bf16[16,24,1,448]{3,1,2,0:T(8,128)(2,1)}), bf16[16,24,1,448]{3,1,2,0:T(8,128)(2,1)S(1)}, u32[]{:S(2)}, u32[]{:S(2)}) async-start(bf16[16,24,1,448]{3,1,2,0:T(8,128)(2,1)} %bitcast.6), calls=%async_computation | async-start | bytes 786432 | tf_op jit(solution)/shard_map/all_to_all | solution.py:71
  48.6 77.5 %reduce-scatter.3.cloned.1.call-start = ((), (), s32[]{:S(2)}) async-start(), calls=%async_computation.6 | async-start | bytes 557056 | tf_op jit(solution)/shard_map/reduce_scatter | solution.py:66
  73.2 14.1 %copy-start.8 = (f32[2,16,8]{1,2,0:T(8,128)S(1)}, f32[2,16,8]{1,2,0:T(8,128)}, u32[]{:S(2)}) copy-start(f32[2,16,8]{1,2,0:T(8,128)} %param.21) | copy-start | bytes 3076
  80.9 21.1 %all-to-all-start.1 = ((bf16[16,24,1,448]{3,1,2,0:T(8,128)(2,1)}), bf16[16,24,1,448]{3,1,2,0:T(8,128)(2,1)S(1)}, u32[]{:S(2)}, u32[]{:S(2)}) async-start(bf16[16,24,1,448]{3,1,2,0:T(8,128)(2,1)} %copy.43), calls=%async_computation.1 | async-start | bytes 786432 | tf_op jit(solution)/shard_map/all_to_all | solution.py:76
  134.3 5.8 %copy-start.1 = (bf16[2,2048,448]{1,2,0:T(8,128)(2,1)S(1)}, bf16[2,2048,448]{1,2,0:T(8,128)(2,1)}, u32[]{:S(2)}) copy-start(bf16[2,2048,448]{1,2,0:T(8,128)(2,1)} %param.18) | copy-start | bytes 11010052
  142.2 33.4 %all-to-all-start.2 = ((bf16[16,24,1,448]{3,1,2,0:T(8,128)(2,1)}), bf16[16,24,1,448]{3,1,2,0:T(8,128)(2,1)S(1)}, u32[]{:S(2)}, u32[]{:S(2)}) async-start(bf16[16,24,1,448]{3,1,2,0:T(8,128)(2,1)} %bitcast.25), calls=%async_computation.3 | async-start | bytes 786432 | tf_op jit(solution)/shard_map/all_to_all | solution.py:71
  151.0 77.8 %reduce-scatter.5.cloned.1.call-start = ((), (), s32[]{:S(2)}) async-start(), calls=%async_computation.7 | async-start | bytes 557056 | tf_op jit(solution)/shard_map/reduce_scatter | solution.py:66
  183.3 21.0 %all-to-all-start.3 = ((bf16[16,24,1,448]{3,1,2,0:T(8,128)(2,1)}), bf16[16,24,1,448]{3,1,2,0:T(8,128)(2,1)S(1)}, u32[]{:S(2)}, u32[]{:S(2)}) async-start(bf16[16,24,1,448]{3,1,2,0:T(8,128)(2,1)} %copy.51), calls=%async_computation.4 | async-start | bytes 786432 | tf_op jit(solution)/shard_map/all_to_all | solution.py:76
Sparse Core Ops, SparseCore 0:
  73.3 52.7 reduce-scatter.2
  175.7 53.1 reduce-scatter.4
where the time goes:
time: 240 us; the launch traced here: 237 us
  waiting for transfers between devices  77.1 us (32%)
  blocking collectives  45.8 us (19%)
  matrix products  45.1 us (19%)
  starting transfers between devices  32.5 us (14%)
  local copies, waits for them, and re-layouts  18.8 us (8%)
  between operations  13.6 us (6%)
  other arithmetic  4.26 us (2%)
    reduce_scatter x2, waiting for transfers between devices, device_step(): lax.psum_scatter(shared_part, 'dp', scatter_dimension=0, tiled=True)  48.1 us
    all_gather x2, blocking collectives, device_step(): gathered = lax.all_gather(ffn_in, 'dp', axis=0, tiled=True)  45.8 us
    all_to_all x2, waiting for transfers between devices, device_step(): returned = lax.all_to_all(expert_out, 'dp', 0, 0, tiled=True)  28.9 us
    all_to_all x2, starting transfers between devices, device_step(): recv_buf = lax.all_to_all(send_buf, 'dp', 0, 0, tiled=True)  19.5 us
    squeeze x1, local copies, waits for them, and re-layouts, device_step(): cache[layer_idx]  14.2 us
    all_to_all x2, starting transfers between devices, device_step(): returned = lax.all_to_all(expert_out, 'dp', 0, 0, tiled=True)  12.8 us
    dot_general x2, matrix products, local_attention(): jnp.einsum('bht,btc->bhc', probs, cache_l[:, :, :LATENT], preferred_eleme...  11.6 us
    sub x2, matrix products, local_attention(): jax.nn.softmax(jnp.where(valid, scores, -jnp.inf), axis=-1)  10.4 us
  transfers between devices with their start and end apart: 6, of which 4 were waited for; matrix products, arithmetic and copies ran while one was open for 8% of the time, Pallas kernels for 0%

commit v1 on v0

v1 whole, which is shorter than its diff:
```python
import functools

import jax
import jax.numpy as jnp
from jax import lax
from jax.experimental import pallas as pl
from jax.experimental.pallas import tpu as pltpu
from jax.sharding import PartitionSpec as P

NORM_EPS = 1e-6
ATT_SCALE = 1.0 / (192.0 ** 0.5)
LATENT = 512
MESH = pl.DeviceIdType.MESH
F32 = jnp.float32
BF16 = jnp.bfloat16


def rms_norm(vals32):
    return vals32 * lax.rsqrt(jnp.mean(vals32 * vals32, axis=-1, keepdims=True) + NORM_EPS)


def dot(lhs, rhs):
    return jnp.dot(lhs, rhs, preferred_element_type=F32)


def dot_t(lhs, rhs):
    return lax.dot_general(lhs, rhs, (((1,), (1,)), ((), ())), preferred_element_type=F32)


def step_kernel(chips, len_ref, x_hbm, cache_hbm, wq_hbm, wo_hbm, ids_hbm, slots_hbm, rw_hbm, w1_hbm, w3_hbm, w2_hbm,
                w1s_hbm, w3s_hbm, w2s_hbm, out_ref,
                x_v, cache_v, wq_v, wo_v, ids_v, slots_v, rw_v, w1_v, w3_v, w2_v, w1s_v, w3s_v, w2s_v,
                rp_all, oh_v, owt_v, g_all, p_buf, r1_buf, s_buf, r2_buf,
                q_v, sc_v, pr_v, o_v, xg_v, u_v,
                loc_sem, cache_sem, ag_send, ag_recv, fwd_send, rs1_send, rs1_recv, rs2_send, rs2_recv):
    layers, bat, kv_dim, seq_len = cache_v.shape
    d_model = x_v.shape[1]
    heads = wq_v.shape[2] // kv_dim
    rows = heads * bat
    n_exp = w1_v.shape[1]
    ff = w1_v.shape[3]
    top_k = ids_v.shape[1]
    group = 2 * chips
    toks = group * bat
    half = chips * bat

    me = lax.axis_index('dp')
    chip = me // 2
    core = me % 2
    other = 1 - core
    q_me = core * chips + chip
    partner = me + 1 - 2 * core

    far_first = (4, 3, 5, 2, 6, 1, 7)
    near_first = (1, 7, 2, 6, 3, 5, 4)

    def chip_at(delta):
        return lax.rem(chip + delta, chips)

    barrier = pltpu.get_barrier_semaphore()
    for delta in far_first:
        pl.semaphore_signal(barrier, inc=1, device_id={'dp': 2 * chip_at(delta) + core}, device_id_type=MESH)
    pl.semaphore_signal(barrier, inc=1, device_id={'dp': partner}, device_id_type=MESH)

    def load(src, dst, idx):
        return pltpu.make_async_copy(src, dst, loc_sem.at[idx])

    small = [load(x_hbm, x_v, 0), load(ids_hbm, ids_v, 1), load(slots_hbm, slots_v, 2), load(rw_hbm, rw_v, 3),
             load(w1s_hbm, w1s_v, 4), load(w3s_hbm, w3s_v, 5), load(w2s_hbm, w2s_v, 6)]
    wq_cp = [load(wq_hbm.at[l], wq_v.at[l], 7 + l) for l in range(layers)]
    wo_cp = [load(wo_hbm.at[l], wo_v.at[l], 9 + l) for l in range(layers)]
    w3_cp = [load(w3_hbm.at[l], w3_v.at[l], 11 + l) for l in range(layers)]
    w1_cp = [load(w1_hbm.at[l], w1_v.at[l], 13 + l) for l in range(layers)]
    w2_cp = [load(w2_hbm.at[l], w2_v.at[l], 15 + l) for l in range(layers)]

    def cache_cp(l, b):
        return pltpu.make_async_copy(cache_hbm.at[l, b], cache_v.at[l, b], cache_sem.at[l, b])

    small[0].start()
    wq_cp[0].start()
    for cp in small[1:4]:
        cp.start()
    for b in range(bat):
        cache_cp(0, b).start()
    for cp in small[4:]:
        cp.start()
    wo_cp[0].start()

    def remote(src, dst, send, recv, dev):
        return pltpu.make_async_remote_copy(src_ref=src, dst_ref=dst, send_sem=send, recv_sem=recv,
                                            device_id={'dp': dev}, device_id_type=MESH)

    def ag_copies(buf, ph):
        mine = buf.at[q_me]
        cps = [remote(mine, mine, ag_send.at[ph, i], ag_recv.at[ph, q_me], 2 * chip_at(delta) + core)
               for i, delta in enumerate(far_first)]
        cps.append(remote(mine, mine, ag_send.at[ph, chips - 1], ag_recv.at[ph, q_me], partner))
        return cps

    def ag_start(buf, ph):
        cps = ag_copies(buf, ph)
        for cp in cps:
            cp.start()
        return cps

    def ag_finish(buf, ph, cps):
        fwd = []
        for i, delta in enumerate(near_first):
            q = core * chips + chip_at(chips - delta)
            cp = remote(buf.at[q], buf.at[q], fwd_send.at[ph, i], ag_recv.at[ph, q], partner)
            cp.wait_recv()
            cp.start()
            fwd.append(cp)
        for delta in (0,) + near_first:
            q = other * chips + chip_at(chips - delta)
            remote(buf.at[q], buf.at[q], fwd_send.at[ph, 0], ag_recv.at[ph, q], partner).wait_recv()
        for cp in cps + fwd:
            cp.wait_send()

    row_tok = lax.rem(lax.broadcasted_iota(jnp.int32, (rows, 1), 0), bat)

    for cp in small[1:4]:
        cp.wait()
    pieces = []
    for l in range(layers):
        pieces.append(jnp.where(slots_v[l] >= 0, ids_v[l] + 1, 0).astype(F32))
    for l in range(layers):
        pieces.append(rw_v[l])
    packed = jnp.concatenate(pieces, axis=0)
    packed = jnp.concatenate([packed, jnp.zeros((2 * layers * top_k, half - bat), F32)], axis=1)
    rp_all[q_me] = pltpu.roll(packed, chip * bat, 1)

    pl.semaphore_wait(barrier, chips)
    rp_cps = ag_start(rp_all, layers)

    small[0].wait()

    def attention(l):
        hidden = rms_norm(x_v[...].astype(F32)).astype(BF16)
        wq_cp[l].wait()
        q = dot(hidden, wq_v[l])
        for hd in range(heads):
            part = q if hd == 0 else pltpu.roll(q, heads * kv_dim - hd * kv_dim, 1)
            q_v[hd * bat:(hd + 1) * bat, :] = part[:, :kv_dim].astype(BF16)
        q_all = q_v[...]
        sc_v[...] = jnp.zeros(sc_v.shape, F32)

        def score_step(g, carry):
            acc = None
            for i in range(4):
                b = 4 * g + i
                cache_cp(l, b).wait()
                qm = q_all * (row_tok == b).astype(F32).astype(BF16)
                term = dot(qm, cache_v[l, b])
                acc = term if acc is None else acc + term
            sc_v[...] += acc
            return carry

        lax.fori_loop(0, bat // 4, score_step, 0)
        if l == 0:
            for cps in (w3_cp, w1_cp, w2_cp):
                cps[0].start()
        lens = jnp.zeros((rows, 1), jnp.int32)
        for b in range(bat):
            lens = jnp.where(row_tok == b, len_ref[b], lens)
        valid = lax.broadcasted_iota(jnp.int32, (rows, seq_len), 1) < lens
        scores = jnp.where(valid, sc_v[...] * ATT_SCALE, -jnp.inf)
        top = jnp.max(scores, axis=1, keepdims=True)
        ex = jnp.exp(scores - top)
        probs = (ex / jnp.sum(ex, axis=1, keepdims=True)).astype(BF16)
        o_v[...] = jnp.zeros(o_v.shape, F32)

        def out_step(g, carry):
            acc = None
            for i in range(4):
                b = 4 * g + i
                pm = probs * (row_tok == b).astype(F32).astype(BF16)
                term = dot_t(pm, cache_v[l, b, 0:LATENT, :])
                acc = term if acc is None else acc + term
            o_v[...] += acc
            return carry

        lax.fori_loop(0, bat // 4, out_step, 0)
        attn = jnp.concatenate([o_v[hd * bat:(hd + 1) * bat, :].astype(BF16) for hd in range(heads)], axis=1)
        wo_cp[l].wait()
        return (x_v[...].astype(F32) + dot_t(attn, wo_v[l])).astype(BF16)

    def build_masks():
        code_w = []
        for k in range(2):
            tot = rp_all[k * chips]
            for j in range(1, chips):
                tot = tot + rp_all[k * chips + j]
            code_w.append(tot)
        code_w = jnp.concatenate(code_w, axis=1)
        base = me * n_exp + 1
        exp_iota = lax.broadcasted_iota(jnp.int32, (n_exp, toks), 0)
        want = (exp_iota + base).astype(F32)
        lane_src = lax.broadcasted_iota(jnp.int32, (group, toks), 1) // bat
        own_src = lane_src == lax.broadcasted_iota(jnp.int32, (group, toks), 0)
        for l in range(layers):
            member = jnp.zeros((n_exp, toks), F32)
            weight = jnp.zeros((n_exp, toks), F32)
            for j in range(top_k):
                hit = code_w[l * top_k + j:l * top_k + j + 1, :] == want
                member = jnp.where(hit, 1.0, member)
                wrow = code_w[(layers + l) * top_k + j:(layers + l) * top_k + j + 1, :]
                weight = jnp.where(hit, wrow, weight)
            onehot = [jnp.where(own_src, member[n:n + 1, :], 0.0) for n in range(n_exp)]
            oh_v[l] = jnp.concatenate(onehot, axis=0).astype(BF16)
            ow = jnp.concatenate([jnp.where(own_src, weight[n:n + 1, :], 0.0) for n in range(n_exp)], axis=0)
            owt = ow.T
            hi = owt.astype(BF16)
            rest = owt - hi.astype(F32)
            mid = rest.astype(BF16)
            low = (rest - mid.astype(F32)).astype(BF16)
            owt_v[l, 0] = hi
            owt_v[l, 1] = mid
            owt_v[l, 2] = low

    def experts(l):
        g_in = g_all[l].reshape(toks, d_model)
        xg_v[...] = dot(oh_v[l], g_in).astype(BF16)
        gate = dot_t(g_in, w3s_v[l])
        up = dot_t(g_in, w1s_v[l])
        shared_h = (jax.nn.silu(gate) * up).astype(BF16)
        shared = dot(shared_h, w2s_v[l])

        for cps in (w3_cp, w1_cp, w2_cp):
            cps[l].wait()

        def pair_step(i, carry):
            for jj in range(2):
                pair = 2 * i + jj
                hid = []
                for e in range(2):
                    n = 2 * pair + e
                    start = pl.multiple_of(n * group, group)
                    xin = xg_v[pl.ds(start, group), :]
                    w31 = jnp.concatenate([w3_v[l, n], w1_v[l, n]], axis=1)
                    both = dot(xin, w31)
                    hid.append((jax.nn.silu(both[:, :ff]) * both[:, ff:]).astype(BF16))
                zero = jnp.zeros((group, ff), BF16)
                lhs = jnp.concatenate([jnp.concatenate([hid[0], zero], axis=1),
                                       jnp.concatenate([zero, hid[1]], axis=1)], axis=0)
                w2p = jnp.concatenate([w2_v[l, 2 * pair], w2_v[l, 2 * pair + 1]], axis=1)
                start = pl.multiple_of(pair * 2 * group, 2 * group)
                u_v[pl.ds(start, 2 * group), :] = dot_t(lhs, w2p).astype(BF16)
            return carry

        lax.fori_loop(0, n_exp // 4, pair_step, 0)
        u_in = u_v[...]
        total = shared + (dot(owt_v[l, 0], u_in) + dot(owt_v[l, 1], u_in) + dot(owt_v[l, 2], u_in))
        p_buf[l] = total.reshape(group, bat, d_model)

    def combine(l):
        first = remote(p_buf.at[l, pl.ds(other * chips, chips)], r1_buf.at[l], rs1_send.at[l], rs1_recv.at[l], partner)
        first.start()
        first.wait_recv()
        s_buf[l] = p_buf[l, pl.ds(core * chips, chips)] + r1_buf[l]
        cps = []
        for i, delta in enumerate(far_first):
            dst = chip_at(delta)
            cps.append(remote(s_buf.at[l, dst], r2_buf.at[l, chip], rs2_send.at[l, i], rs2_recv.at[l, chip], 2 * dst + core))
        for cp in cps:
            cp.start()
        r2_buf[l, chip] = s_buf[l, chip]
        for i, delta in enumerate(near_first):
            src = chip_at(chips - delta)
            remote(s_buf.at[l, src], r2_buf.at[l, src], rs2_send.at[l, 0], rs2_recv.at[l, src], partner).wait_recv()
        tot = r2_buf[l, 0]
        for j in range(1, chips):
            tot = tot + r2_buf[l, j]
        first.wait_send()
        for cp in cps:
            cp.wait_send()
        return tot

    for l in range(layers):
        resid = attention(l)
        g_all[l, q_me] = rms_norm(resid.astype(F32)).astype(BF16)
        cps = ag_start(g_all.at[l], l)
        if l == 0:
            for cp in small[4:]:
                cp.wait()
            wq_cp[1].start()
            for b in range(bat):
                cache_cp(1, b).start()
            for cp_list in (wo_cp, w3_cp, w1_cp, w2_cp):
                cp_list[1].start()
            ag_finish(rp_all, layers, rp_cps)
            build_masks()
        ag_finish(g_all.at[l], l, cps)
        experts(l)
        x_v[...] = (resid.astype(F32) + combine(l)).astype(BF16)
    out_ref[...] = x_v[...]


def solution(mesh):
    group = mesh.shape['dp']
    chips = group // 2
    tok_axes = ('replica', 'dp')
    in_specs = (
        P(tok_axes, None), P(tok_axes), P(None, tok_axes, None, None),
        P(None, None, None), P(None, None, None),
        P(None, tok_axes, None), P(None, tok_axes, None), P(None, tok_axes, None),
        P(None, 'dp', None, None), P(None, 'dp', None, None), P(None, 'dp', None, None),
        P(None, None, 'dp'), P(None, None, 'dp'), P(None, 'dp', None),
    )

    def device_step(x, lengths, cache, w_q, w_o, expert_ids, slots, route_w, w1_exp, w3_exp, w2_exp, w1_sh, w3_sh, w2_sh):
        bat, d_model = x.shape
        layers, _, seq_len, kv_dim = cache.shape
        n_exp, ff = w1_exp.shape[1], w1_exp.shape[3]
        top_k = expert_ids.shape[2]
        heads = w_q.shape[2] // kv_dim
        assert max(1, (2 * bat * top_k) // (n_exp * group)) == 1 and layers == 2 and chips == 8
        swap = lambda a: jnp.swapaxes(a, -1, -2)
        args = (lengths, x, swap(cache), w_q, swap(w_o), swap(expert_ids), swap(slots), swap(route_w),
                w1_exp, w3_exp, swap(w2_exp), swap(w1_sh), swap(w3_sh), w2_sh)
        vm = lambda a: pltpu.VMEM(a.shape, a.dtype)
        toks = group * bat
        dma = pltpu.SemaphoreType.DMA
        scratch = [vm(a) for a in args[1:]] + [
            pltpu.VMEM((group, 2 * layers * top_k, chips * bat), F32),
            pltpu.VMEM((layers, n_exp * group, toks), BF16),
            pltpu.VMEM((layers, 3, toks, n_exp * group), BF16),
            pltpu.VMEM((layers, group, bat, d_model), BF16),
            pltpu.VMEM((layers, group, bat, d_model), F32),
            pltpu.VMEM((layers, chips, bat, d_model), F32),
            pltpu.VMEM((layers, chips, bat, d_model), F32),
            pltpu.VMEM((layers, chips, bat, d_model), F32),
            pltpu.VMEM((heads * bat, kv_dim), BF16),
            pltpu.VMEM((heads * bat, seq_len), F32),
            pltpu.VMEM((heads * bat, seq_len), BF16),
            pltpu.VMEM((heads * bat, LATENT), F32),
            pltpu.VMEM((n_exp * group, d_model), BF16),
            pltpu.VMEM((n_exp * group, d_model), BF16),
            dma((17,)), dma((layers, bat)),
            dma((layers + 1, chips)), dma((layers + 1, group)), dma((layers + 1, chips)),
            dma((layers,)), dma((layers,)), dma((layers, chips)), dma((layers, chips)),
        ]
        return pl.pallas_call(
            functools.partial(step_kernel, chips),
            out_shape=jax.ShapeDtypeStruct(x.shape, x.dtype),
            in_specs=[pl.BlockSpec(memory_space=pltpu.SMEM)] + [pl.BlockSpec(memory_space=pl.ANY)] * (len(args) - 1),
            out_specs=pl.BlockSpec(memory_space=pltpu.VMEM),
            scratch_shapes=scratch,
            compiler_params=pltpu.CompilerParams(collective_id=0, has_side_effects=True, vmem_limit_bytes=67043328),
        )(*args)

    return jax.shard_map(device_step, mesh=mesh, in_specs=in_specs, out_specs=P(tok_axes, None), check_vma=False)
```

time: 240 us -> 68.5 us (0.29); the launches traced: 237 us -> 68.3 us
  waiting for transfers between devices: 77.1 us -> 0 us
  Pallas kernels: 0 us -> 67 us
  blocking collectives: 45.8 us -> 0 us
  matrix products: 45.1 us -> 0 us
  starting transfers between devices: 32.5 us -> 0 us
  local copies, waits for them, and re-layouts: 18.8 us -> 1.32 us
  between operations: 13.6 us -> 0.01 us
  other arithmetic: 4.26 us -> 0 us
    pallas_call x0 -> x1, Pallas kernels: none -> 67 us  [device_step(): pl.pallas_call(functools.partial(step_kernel, chips), out_shape=jax.Shape...]
    reduce_scatter x2 -> x0, waiting for transfers between devices: 48.1 us -> none  [device_step(): lax.psum_scatter(shared_part, 'dp', scatter_dimension=0, tiled=True)]
    all_gather x2 -> x0, blocking collectives: 45.8 us -> none  [device_step(): gathered = lax.all_gather(ffn_in, 'dp', axis=0, tiled=True)]
    dot_general x18 -> x0, matrix products: 34.7 us -> none  [the longest x2 11.6 us: local_attention(): jnp.einsum('bht,btc->bhc', probs, cache_l[:, :, :LATENT], preferred_eleme...]
    all_to_all x4 -> x0, starting transfers between devices: 32.3 us -> none  [the longest x2 19.5 us: device_step(): recv_buf = lax.all_to_all(send_buf, 'dp', 0, 0, tiled=True)]
    all_to_all x4 -> x0, waiting for transfers between devices: 28.9 us -> none  [the longest x2 28.9 us: device_step(): returned = lax.all_to_all(expert_out, 'dp', 0, 0, tiled=True)]
    squeeze x1 -> x0, local copies, waits for them, and re-layouts: 14.2 us -> none  [device_step(): cache[layer_idx]]
    sub x2 -> x0, matrix products: 10.4 us -> none  [local_attention(): jax.nn.softmax(jnp.where(valid, scores, -jnp.inf), axis=-1)]
  transfers between devices with their start and end apart: 6 -> 0, of which waited for: 4 -> 0; matrix products, arithmetic and copies ran while one was open for 8% -> 0% of each run, Pallas kernels for 0% -> 0%
where the time goes in v1:
time: 68.5 us; the launch traced here: 68.3 us
  Pallas kernels  67 us (98%)
  local copies, waits for them, and re-layouts  1.32 us (2%)
    pallas_call x1, Pallas kernels, device_step(): pl.pallas_call(functools.partial(step_kernel, chips), out_shape=jax.Shape...  67 us

profile of v1, /device:TPU:21, one launch (start us, length us, event | category | flops | bytes accessed | tf_op | source)
XLA Modules:
  0.0 68.3 jit_solution(16434212672113122913)
XLA Ops:
  0.0 67.0 %shard_map.136 = bf16[16,448]{1,0:T(8,128)(2,1)} custom-call(s32[16]{0:T(128)} %len_ref.1, bf16[16,448]{1,0:T(8,128)(2,1)} %x_hbm.1, bf16[2,16,576,512]{3,2,1,0:T(8,128)(2,1)} %bitcast.8, bf16[2,448,2304]{2,1,0:T(8,128)(2,1)} %wq_hbm.1, bf16[2,448,2048]{2,1,0:T(8,128)(2,1)} %bitcast.10, s32[2,8,16]{2,1,0:T(8,128)} %bitcast.13, s32[2,8,16]{2,1,0:T(8,128)} %bitcast.14, ...), custom_call_target="tpu_custom_call" | custom-call | tf_op jit(solution)/shard_map/pallas_call | solution.py:343
  67.0 1.3 %copy.16 = bf16[16,448]{1,0:T(8,128)(2,1)} copy(bf16[16,448]{1,0:T(8,128)(2,1)} %shard_map.136) | data formatting | bytes 28672

commit v2 on v1

v2 whole, which is shorter than its diff:
```python
import functools

import jax
import jax.numpy as jnp
from jax import lax
from jax.experimental import pallas as pl
from jax.experimental.pallas import tpu as pltpu
from jax.sharding import PartitionSpec as P

NORM_EPS = 1e-6
ATT_SCALE = 1.0 / (192.0 ** 0.5)
LATENT = 512
MESH = pl.DeviceIdType.MESH
F32 = jnp.float32
BF16 = jnp.bfloat16


def rms_norm(vals32):
    return vals32 * lax.rsqrt(jnp.mean(vals32 * vals32, axis=-1, keepdims=True) + NORM_EPS)


def dot(lhs, rhs):
    return jnp.dot(lhs, rhs, preferred_element_type=F32)


def dot_t(lhs, rhs):
    return lax.dot_general(lhs, rhs, (((1,), (1,)), ((), ())), preferred_element_type=F32)


def step_kernel(chips, len_ref, x_hbm, cache_hbm, wq_hbm, wo_hbm, ids_hbm, slots_hbm, rw_hbm, w1_hbm, w3_hbm, w2_hbm,
                w1s_hbm, w3s_hbm, w2s_hbm, out_ref,
                x_v, cache_v, wq_v, wo_v, ids_v, slots_v, rw_v, w1_v, w3_v, w2_v, w1s_v, w3s_v, w2s_v,
                rp_all, oh_v, owt_v, g_all, p_buf, own_buf, r1_buf, s_buf, r2_buf,
                xr_v, wot_v, q_v, sc_v, o_v, xg_v, u_v, sh_v,
                loc_sem, cache_sem, ag_send, ag_recv, fwd_send, rs1_send, rs1_recv, rs2_send, rs2_recv):
    layers, bat, kv_dim, seq_len = cache_v.shape
    d_model = x_v.shape[1]
    heads = wq_v.shape[2] // kv_dim
    n_exp = w1_v.shape[1]
    ff = w1_v.shape[3]
    top_k = ids_v.shape[1]
    group = 2 * chips
    hb = bat // 2
    rows = heads * hb
    toks = group * hb
    half = chips * hb
    quad = 4

    me = lax.axis_index('dp')
    chip = me // 2
    core = me % 2
    other = 1 - core
    q_me = core * chips + chip
    partner = me + 1 - 2 * core

    far_first = (4, 3, 5, 2, 6, 1, 7)
    near_first = (1, 7, 2, 6, 3, 5, 4)

    def chip_at(delta):
        return lax.rem(chip + delta, chips)

    barrier = pltpu.get_barrier_semaphore()
    for delta in far_first:
        pl.semaphore_signal(barrier, inc=1, device_id={'dp': 2 * chip_at(delta) + core}, device_id_type=MESH)
    pl.semaphore_signal(barrier, inc=1, device_id={'dp': partner}, device_id_type=MESH)

    def load(src, dst, idx):
        return pltpu.make_async_copy(src, dst, loc_sem.at[idx])

    small = [load(x_hbm, x_v, 0), load(ids_hbm, ids_v, 1), load(slots_hbm, slots_v, 2), load(rw_hbm, rw_v, 3),
             load(w1s_hbm, w1s_v, 4), load(w3s_hbm, w3s_v, 5), load(w2s_hbm, w2s_v, 6)]
    wq_cp = [load(wq_hbm.at[l], wq_v.at[l], 7 + l) for l in range(layers)]
    wo_cp = [load(wo_hbm.at[l], wo_v.at[l], 9 + l) for l in range(layers)]
    w3_cp = [load(w3_hbm.at[l], w3_v.at[l], 11 + l) for l in range(layers)]
    w1_cp = [load(w1_hbm.at[l], w1_v.at[l], 13 + l) for l in range(layers)]
    w2_cp = [load(w2_hbm.at[l], w2_v.at[l], 15 + l) for l in range(layers)]
    cache_cp = [[pltpu.make_async_copy(cache_hbm.at[l, pl.ds(quad * c, quad)], cache_v.at[l, pl.ds(quad * c, quad)],
                                       cache_sem.at[l, c]) for c in range(bat // quad)] for l in range(layers)]

    small[0].start()
    wq_cp[0].start()
    for cp in small[1:4]:
        cp.start()
    cache_cp[0][0].start()
    wo_cp[0].start()
    for cp in cache_cp[0][1:]:
        cp.start()
    for cp in small[4:]:
        cp.start()

    def remote(src, dst, send, recv, dev):
        return pltpu.make_async_remote_copy(src_ref=src, dst_ref=dst, send_sem=send, recv_sem=recv,
                                            device_id={'dp': dev}, device_id_type=MESH)

    def ag_start(buf, ph):
        mine = buf.at[q_me]
        cps = [remote(mine, mine, ag_send.at[ph, i], ag_recv.at[ph, q_me], 2 * chip_at(delta) + core)
               for i, delta in enumerate(far_first)]
        cps.append(remote(mine, mine, ag_send.at[ph, chips - 1], ag_recv.at[ph, q_me], partner))
        for cp in cps:
            cp.start()
        return cps

    def ag_finish(buf, ph):
        fwd = []
        for i, delta in enumerate(near_first):
            q = core * chips + chip_at(chips - delta)
            cp = remote(buf.at[q], buf.at[q], fwd_send.at[ph, i], ag_recv.at[ph, q], partner)
            cp.wait_recv()
            cp.start()
            fwd.append(cp)
        for delta in (0,) + near_first:
            q = other * chips + chip_at(chips - delta)
            remote(buf.at[q], buf.at[q], fwd_send.at[ph, 0], ag_recv.at[ph, q], partner).wait_recv()
        return fwd

    for cp in small[1:4]:
        cp.wait()
    pieces = []
    for l in range(layers):
        pieces.append(jnp.where(slots_v[l] >= 0, ids_v[l] + 1, 0).astype(F32))
    for l in range(layers):
        pieces.append(rw_v[l])
    packed = jnp.concatenate(pieces, axis=0)
    packed = jnp.concatenate([packed, jnp.zeros((2 * layers * top_k, toks - bat), F32)], axis=1)
    lane = lax.broadcasted_iota(jnp.int32, packed.shape, 1)
    rp_all[q_me, 0] = pltpu.roll(jnp.where(lane < hb, packed, 0.0), q_me * hb, 1)
    second = jnp.where(lane < hb, pltpu.roll(packed, toks - hb, 1), 0.0)
    rp_all[q_me, 1] = pltpu.roll(second, q_me * hb, 1)

    pl.semaphore_wait(barrier, chips)
    sends = ag_start(rp_all, 2 * layers)

    small[0].wait()
    xr_v[...] = x_v[...].astype(F32).reshape(2, hb, d_model)

    def transpose_wo(l):
        wo_cp[l].wait()
        for k in range(heads * LATENT // 128):
            wot_v[l, 128 * k:128 * (k + 1), :] = wo_v[l, :, 128 * k:128 * (k + 1)].T

    def attention(l, hf):
        hidden = rms_norm(xr_v[hf]).astype(BF16)
        if hf == 0:
            wq_cp[l].wait()
        q = dot(hidden, wq_v[l])
        for hd in range(heads):
            part = q if hd == 0 else pltpu.roll(q, heads * kv_dim - hd * kv_dim, 1)
            for k in range(q_v.shape[0]):
                q_v[k, pl.ds(hd, hb, stride=heads), :] = part[:, 128 * k:128 * (k + 1)]
        for c in range(2):
            cache_cp[l][2 * hf + c].wait()
            for i in range(quad):
                b = quad * c + i
                qb = jnp.concatenate([q_v[k, heads * b:heads * (b + 1), :] for k in range(q_v.shape[0])], axis=1)
                qb = qb[:, :kv_dim].astype(BF16)
                sc_v[heads * b:heads * (b + 1), :] = dot(qb, cache_v[l, hf * hb + b])
            if l == 0 and hf == 0 and c == 0:
                transpose_wo(0)
        if l == 0 and hf == 0:
            for cps in (w3_cp, w1_cp, w2_cp):
                cps[0].start()
        row_tok = lax.broadcasted_iota(jnp.int32, (rows, 1), 0) // heads
        lens = jnp.zeros((rows, 1), jnp.int32)
        for b in range(hb):
            lens = jnp.where(row_tok == b, len_ref[hf * hb + b], lens)
        valid = lax.broadcasted_iota(jnp.int32, (rows, seq_len), 1) < lens
        scores = jnp.where(valid, sc_v[...] * ATT_SCALE, -jnp.inf)
        top = jnp.max(scores, axis=1, keepdims=True)
        ex = jnp.exp(scores - top)
        probs = ex / jnp.sum(ex, axis=1, keepdims=True)
        sc_v[...] = probs
        for b in range(hb):
            pb = sc_v[heads * b:heads * (b + 1), :].astype(BF16)
            ob = dot_t(pb, cache_v[l, hf * hb + b, 0:LATENT, :])
            for k in range(o_v.shape[0]):
                o_v[k, heads * b:heads * (b + 1), :] = ob[:, 128 * k:128 * (k + 1)]
        attn = jnp.concatenate([o_v[k, pl.ds(hd, hb, stride=heads), :] for hd in range(heads)
                                for k in range(o_v.shape[0])], axis=1).astype(BF16)
        proj = jnp.concatenate([dot(attn, wot_v[l, :, 0:256]), dot(attn, wot_v[l, :, 256:d_model])], axis=1)
        resid = (xr_v[hf] + proj).astype(BF16).astype(F32)
        xr_v[hf] = resid
        g_all[2 * l + hf, q_me] = rms_norm(resid).astype(BF16)

    def build_masks(l):
        base = me * n_exp + 1
        want = (lax.broadcasted_iota(jnp.int32, (n_exp, toks), 0) + base).astype(F32)
        lane_src = lax.broadcasted_iota(jnp.int32, (group, toks), 1) // hb
        own_src = lane_src == lax.broadcasted_iota(jnp.int32, (group, toks), 0)
        for hf in range(2):
            code = rp_all[0, hf, l * top_k:(l + 1) * top_k, :]
            wval = rp_all[0, hf, (layers + l) * top_k:(layers + l + 1) * top_k, :]
            for j in range(1, group):
                code = code + rp_all[j, hf, l * top_k:(l + 1) * top_k, :]
                wval = wval + rp_all[j, hf, (layers + l) * top_k:(layers + l + 1) * top_k, :]
            member = jnp.zeros((n_exp, toks), F32)
            weight = jnp.zeros((n_exp, toks), F32)
            for j in range(top_k):
                hit = code[j:j + 1, :] == want
                member = jnp.where(hit, 1.0, member)
                weight = jnp.where(hit, wval[j:j + 1, :], weight)
            onehot = [jnp.where(own_src, member[n:n + 1, :], 0.0) for n in range(n_exp)]
            oh_v[l, hf] = jnp.concatenate(onehot, axis=0).astype(BF16)
            ow = jnp.concatenate([jnp.where(own_src, weight[n:n + 1, :], 0.0) for n in range(n_exp)], axis=0)
            owt = ow.T
            hi = owt.astype(BF16)
            rest = owt - hi.astype(F32)
            mid = rest.astype(BF16)
            low = (rest - mid.astype(F32)).astype(BF16)
            owt_v[l, hf, 0] = hi
            owt_v[l, hf, 1] = mid
            owt_v[l, hf, 2] = low

    unroll = 4

    def experts(l, hf, between=None):
        ph = 2 * l + hf
        g_in = g_all[ph].reshape(toks, d_model)
        xg_v[...] = dot(oh_v[l, hf], g_in).astype(BF16)
        gate = dot_t(g_in, w3s_v[l])
        up = dot_t(g_in, w1s_v[l])
        shared_h = (jax.nn.silu(gate) * up).astype(BF16)
        sh_v[...] = dot(shared_h, w2s_v[l])
        if hf == 0:
            for cps in (w3_cp, w1_cp, w2_cp):
                cps[l].wait()

        def first_layer(pair):
            hid = []
            for e in range(2):
                n = 2 * pair + e
                start = pl.multiple_of(n * group, group)
                xin = xg_v[pl.ds(start, group), :]
                w31 = jnp.concatenate([w3_v[l, n], w1_v[l, n]], axis=1)
                both = dot(xin, w31)
                hid.append((jax.nn.silu(both[:, :ff]) * both[:, ff:]).astype(BF16))
            zero = jnp.zeros((group, ff), BF16)
            return jnp.concatenate([jnp.concatenate([hid[0], zero], axis=1),
                                    jnp.concatenate([zero, hid[1]], axis=1)], axis=0)

        def second_layer(pair, lhs):
            w2p = jnp.concatenate([w2_v[l, 2 * pair], w2_v[l, 2 * pair + 1]], axis=1)
            start = pl.multiple_of(pair * 2 * group, 2 * group)
            u_v[pl.ds(start, 2 * group), :] = dot_t(lhs, w2p).astype(BF16)

        def pair_step(i, carry):
            ready = first_layer(unroll * i)
            for jj in range(unroll):
                pair = unroll * i + jj
                coming = first_layer(pair + 1) if jj < unroll - 1 else None
                second_layer(pair, ready)
                ready = coming
            return carry

        steps = n_exp // (2 * unroll)
        lax.fori_loop(0, 1, pair_step, 0)
        if between is not None:
            between()
        lax.fori_loop(1, steps, pair_step, 0)

        def part(k):
            sel = pl.ds(pl.multiple_of(k * half, half), half)
            u_in = u_v[...]
            return sh_v[sel, :] + (dot(owt_v[l, hf, 0, sel, :], u_in) + dot(owt_v[l, hf, 1, sel, :], u_in)
                                   + dot(owt_v[l, hf, 2, sel, :], u_in))

        p_buf[ph] = part(other).reshape(chips, hb, d_model)
        first = remote(p_buf.at[ph], r1_buf.at[ph], rs1_send.at[ph], rs1_recv.at[ph], partner)
        first.start()
        own_buf[ph] = part(core).reshape(chips, hb, d_model)
        return first

    def second_stage(l, hf, first):
        ph = 2 * l + hf
        first.wait_recv()
        s_buf[ph] = own_buf[ph] + r1_buf[ph]
        cps = [first]
        for i, delta in enumerate(far_first):
            dst = chip_at(delta)
            cp = remote(s_buf.at[ph, dst], r2_buf.at[ph, chip], rs2_send.at[ph, i], rs2_recv.at[ph, chip], 2 * dst + core)
            cp.start()
            cps.append(cp)
        r2_buf[ph, chip] = s_buf[ph, chip]
        return cps

    def finish(l, hf):
        ph = 2 * l + hf
        for i, delta in enumerate(near_first):
            src = chip_at(chips - delta)
            remote(s_buf.at[ph, src], r2_buf.at[ph, src], rs2_send.at[ph, 0], rs2_recv.at[ph, src], partner).wait_recv()
        tot = r2_buf[ph, 0]
        for j in range(1, chips):
            tot = tot + r2_buf[ph, j]
        xr_v[hf] = (xr_v[hf] + tot).astype(BF16).astype(F32)

    for l in range(layers):
        for hf in range(2):
            if l > 0:
                finish(l - 1, hf)
            attention(l, hf)
            sends += ag_start(g_all.at[2 * l + hf], 2 * l + hf)
            if l == 0 and hf == 0:
                wq_cp[1].start()
                for cp in cache_cp[1]:
                    cp.start()
        if l == 0:
            for cp_list in (wo_cp, w3_cp, w1_cp, w2_cp):
                cp_list[1].start()
            for cp in small[4:]:
                cp.wait()
            sends += ag_finish(rp_all, 2 * layers)
            build_masks(0)
        sends += ag_finish(g_all.at[2 * l], 2 * l)
        first_a = experts(l, 0)
        sends += ag_finish(g_all.at[2 * l + 1], 2 * l + 1)
        later = []
        first_b = experts(l, 1, lambda: later.extend(second_stage(l, 0, first_a)))
        if l == 0:
            build_masks(1)
            transpose_wo(1)
        sends += later + second_stage(l, 1, first_b)
    for hf in range(2):
        finish(layers - 1, hf)
    for cp in sends:
        cp.wait_send()
    out_ref[...] = xr_v[...].reshape(bat, d_model).astype(BF16)


def solution(mesh):
    group = mesh.shape['dp']
    chips = group // 2
    tok_axes = ('replica', 'dp')
    in_specs = (
        P(tok_axes, None), P(tok_axes), P(None, tok_axes, None, None),
        P(None, None, None), P(None, None, None),
        P(None, tok_axes, None), P(None, tok_axes, None), P(None, tok_axes, None),
        P(None, 'dp', None, None), P(None, 'dp', None, None), P(None, 'dp', None, None),
        P(None, None, 'dp'), P(None, None, 'dp'), P(None, 'dp', None),
    )

    def device_step(x, lengths, cache, w_q, w_o, expert_ids, slots, route_w, w1_exp, w3_exp, w2_exp, w1_sh, w3_sh, w2_sh):
        bat, d_model = x.shape
        layers, _, seq_len, kv_dim = cache.shape
        n_exp, ff = w1_exp.shape[1], w1_exp.shape[3]
        top_k = expert_ids.shape[2]
        heads = w_q.shape[2] // kv_dim
        assert max(1, (2 * bat * top_k) // (n_exp * group)) == 1 and layers == 2 and chips == 8
        swap = lambda a: jnp.swapaxes(a, -1, -2)
        args = (lengths, x, swap(cache), w_q, swap(w_o), swap(expert_ids), swap(slots), swap(route_w),
                w1_exp, w3_exp, swap(w2_exp), swap(w1_sh), swap(w3_sh), w2_sh)
        vm = lambda a: pltpu.VMEM(a.shape, a.dtype)
        dma = pltpu.SemaphoreType.DMA
        phs = 2 * layers
        hb = bat // 2
        toks = group * hb
        slots_n = n_exp * group
        scratch = [vm(a) for a in args[1:]] + [
            pltpu.VMEM((group, 2, 2 * layers * top_k, toks), F32),
            pltpu.VMEM((layers, 2, slots_n, toks), BF16),
            pltpu.VMEM((layers, 2, 3, toks, slots_n), BF16),
            pltpu.VMEM((phs, group, hb, d_model), BF16),
            pltpu.VMEM((phs, chips, hb, d_model), F32),
            pltpu.VMEM((phs, chips, hb, d_model), F32),
            pltpu.VMEM((phs, chips, hb, d_model), F32),
            pltpu.VMEM((phs, chips, hb, d_model), F32),
            pltpu.VMEM((phs, chips, hb, d_model), F32),
            pltpu.VMEM((2, hb, d_model), F32),
            pltpu.VMEM((layers, heads * LATENT, d_model), BF16),
            pltpu.VMEM((-(-kv_dim // 128), heads * hb, 128), F32),
            pltpu.VMEM((heads * hb, seq_len), F32),
            pltpu.VMEM((LATENT // 128, heads * hb, 128), F32),
            pltpu.VMEM((slots_n, d_model), BF16),
            pltpu.VMEM((slots_n, d_model), BF16),
            pltpu.VMEM((toks, d_model), F32),
            dma((17,)), dma((layers, bat // 4)),
            dma((phs + 1, chips)), dma((phs + 1, group)), dma((phs + 1, chips)),
            dma((phs,)), dma((phs,)), dma((phs, chips)), dma((phs, chips)),
        ]
        return pl.pallas_call(
            functools.partial(step_kernel, chips),
            out_shape=jax.ShapeDtypeStruct(x.shape, x.dtype),
            in_specs=[pl.BlockSpec(memory_space=pltpu.SMEM)] + [pl.BlockSpec(memory_space=pl.ANY)] * (len(args) - 1),
            out_specs=pl.BlockSpec(memory_space=pltpu.VMEM),
            scratch_shapes=scratch,
            compiler_params=pltpu.CompilerParams(collective_id=0, has_side_effects=True, vmem_limit_bytes=67043328),
        )(*args)

    return jax.shard_map(device_step, mesh=mesh, in_specs=in_specs, out_specs=P(tok_axes, None), check_vma=False)
```

time: 68.5 us -> 57.7 us (0.84)
  Pallas kernels: 67 us -> 56.1 us
    pallas_call x1, Pallas kernels: 67 us -> 56.1 us  [device_step(): pl.pallas_call(functools.partial(step_kernel, chips), out_shape=jax.Shape...]
where the time goes in v2:
time: 57.7 us; the launch traced here: 57.5 us
  Pallas kernels  56.1 us (97%)
  local copies, waits for them, and re-layouts  1.32 us (2%)
    pallas_call x1, Pallas kernels, device_step(): pl.pallas_call(functools.partial(step_kernel, chips), out_shape=jax.Shape...  56.1 us
    unnamed x1, local copies, waits for them, and re-layouts  1.32 us

profile of v2, /device:TPU:21, one launch (start us, length us, event | category | flops | bytes accessed | tf_op | source)
XLA Modules:
  0.0 57.5 jit_solution(8426093343420312973)
XLA Ops:
  0.0 56.1 %shard_map.136 = bf16[16,448]{1,0:T(8,128)(2,1)} custom-call(s32[16]{0:T(128)} %len_ref.1, bf16[16,448]{1,0:T(8,128)(2,1)} %x_hbm.1, bf16[2,16,576,512]{3,2,1,0:T(8,128)(2,1)} %bitcast.8, bf16[2,448,2304]{2,1,0:T(8,128)(2,1)} %wq_hbm.1, bf16[2,448,2048]{2,1,0:T(8,128)(2,1)} %bitcast.10, s32[2,8,16]{2,1,0:T(8,128)} %bitcast.13, s32[2,8,16]{2,1,0:T(8,128)} %bitcast.14, ...), custom_call_target="tpu_custom_call" | custom-call | tf_op jit(solution)/shard_map/pallas_call | solution.py:379
  56.1 1.3 %copy.16 = bf16[16,448]{1,0:T(8,128)(2,1)} copy(bf16[16,448]{1,0:T(8,128)(2,1)} %shard_map.136) | data formatting | bytes 28672

commit v3 on v2

--- a/solution.py
+++ b/solution.py
@@ -27,12 +27,12 @@
     return lax.dot_general(lhs, rhs, (((1,), (1,)), ((), ())), preferred_element_type=F32)
 
 
-def step_kernel(chips, len_ref, x_hbm, cache_hbm, wq_hbm, wo_hbm, ids_hbm, slots_hbm, rw_hbm, w1_hbm, w3_hbm, w2_hbm,
+def step_kernel(chips, len_hbm, x_hbm, cache_hbm, wq_hbm, wo_hbm, ids_hbm, slots_hbm, rw_hbm, w1_hbm, w3_hbm, w2_hbm,
                 w1s_hbm, w3s_hbm, w2s_hbm, out_ref,
-                x_v, cache_v, wq_v, wo_v, ids_v, slots_v, rw_v, w1_v, w3_v, w2_v, w1s_v, w3s_v, w2s_v,
+                len_ref, x_v, cache_v, wq_v, wo_v, ids_v, slots_v, rw_v, w1_v, w3_v, w2_v, w1s_v, w3s_v, w2s_v,
                 rp_all, oh_v, owt_v, g_all, p_buf, own_buf, r1_buf, s_buf, r2_buf,
                 xr_v, wot_v, q_v, sc_v, o_v, xg_v, u_v, sh_v,
-                loc_sem, cache_sem, ag_send, ag_recv, fwd_send, rs1_send, rs1_recv, rs2_send, rs2_recv):
+                loc_sem, cache_sem, ag_send, ag_recv, rs1_send, rs1_recv, rs2_send, rs2_recv):
     layers, bat, kv_dim, seq_len = cache_v.shape
     d_model = x_v.shape[1]
     heads = wq_v.shape[2] // kv_dim
@@ -59,11 +59,6 @@
     def chip_at(delta):
         return lax.rem(chip + delta, chips)
 
-    barrier = pltpu.get_barrier_semaphore()
-    for delta in far_first:
-        pl.semaphore_signal(barrier, inc=1, device_id={'dp': 2 * chip_at(delta) + core}, device_id_type=MESH)
-    pl.semaphore_signal(barrier, inc=1, device_id={'dp': partner}, device_id_type=MESH)
-
     def load(src, dst, idx):
         return pltpu.make_async_copy(src, dst, loc_sem.at[idx])
 
@@ -79,14 +74,21 @@
 
     small[0].start()
     wq_cp[0].start()
+    len_cp = pltpu.make_async_copy(len_hbm, len_ref, loc_sem.at[17])
     for cp in small[1:4]:
         cp.start()
     cache_cp[0][0].start()
     wo_cp[0].start()
     for cp in cache_cp[0][1:]:
         cp.start()
+    len_cp.start()
     for cp in small[4:]:
         cp.start()
+
+    barrier = pltpu.get_barrier_semaphore()
+    for delta in far_first:
+        pl.semaphore_signal(barrier, inc=1, device_id={'dp': 2 * chip_at(delta) + core}, device_id_type=MESH)
+    pl.semaphore_signal(barrier, inc=1, device_id={'dp': partner}, device_id_type=MESH)
 
     def remote(src, dst, send, recv, dev):
         return pltpu.make_async_remote_copy(src_ref=src, dst_ref=dst, send_sem=send, recv_sem=recv,
@@ -94,39 +96,30 @@
 
     def ag_start(buf, ph):
         mine = buf.at[q_me]
-        cps = [remote(mine, mine, ag_send.at[ph, i], ag_recv.at[ph, q_me], 2 * chip_at(delta) + core)
+        cps = [remote(mine, mine, ag_send.at[ph, i], ag_recv.at[ph, chip], 2 * chip_at(delta) + core)
                for i, delta in enumerate(far_first)]
-        cps.append(remote(mine, mine, ag_send.at[ph, chips - 1], ag_recv.at[ph, q_me], partner))
         for cp in cps:
             cp.start()
         return cps
 
     def ag_finish(buf, ph):
-        fwd = []
         for i, delta in enumerate(near_first):
-            q = core * chips + chip_at(chips - delta)
-            cp = remote(buf.at[q], buf.at[q], fwd_send.at[ph, i], ag_recv.at[ph, q], partner)
-            cp.wait_recv()
-            cp.start()
-            fwd.append(cp)
-        for delta in (0,) + near_first:
-            q = other * chips + chip_at(chips - delta)
-            remote(buf.at[q], buf.at[q], fwd_send.at[ph, 0], ag_recv.at[ph, q], partner).wait_recv()
-        return fwd
+            src = chip_at(chips - delta)
+            q = core * chips + src
+            remote(buf.at[q], buf.at[q], ag_send.at[ph, 0], ag_recv.at[ph, src], partner).wait_recv()
+        mine = buf.at[pl.ds(core * chips, chips)]
+        theirs = buf.at[pl.ds(other * chips, chips)]
+        cp = remote(mine, mine, ag_send.at[ph, chips - 1], ag_recv.at[ph, chips], partner)
+        cp.start()
+        remote(theirs, theirs, ag_send.at[ph, chips - 1], ag_recv.at[ph, chips], partner).wait_recv()
+        return [cp]
 
     for cp in small[1:4]:
         cp.wait()
-    pieces = []
-    for l in range(layers):
-        pieces.append(jnp.where(slots_v[l] >= 0, ids_v[l] + 1, 0).astype(F32))
-    for l in range(layers):
-        pieces.append(rw_v[l])
-    packed = jnp.concatenate(pieces, axis=0)
-    packed = jnp.concatenate([packed, jnp.zeros((2 * layers * top_k, toks - bat), F32)], axis=1)
-    lane = lax.broadcasted_iota(jnp.int32, packed.shape, 1)
-    rp_all[q_me, 0] = pltpu.roll(jnp.where(lane < hb, packed, 0.0), q_me * hb, 1)
-    second = jnp.where(lane < hb, pltpu.roll(packed, toks - hb, 1), 0.0)
-    rp_all[q_me, 1] = pltpu.roll(second, q_me * hb, 1)
+    pieces = [jnp.where(slots_v[l] >= 0, ids_v[l] + 1, 0).astype(F32) for l in range(layers)]
+    pieces += [rw_v[l] for l in range(layers)]
+    pieces.append(jnp.zeros((top_k, toks - 2 * layers * bat), F32))
+    rp_all[q_me] = jnp.concatenate(pieces, axis=1)
 
     pl.semaphore_wait(barrier, chips)
     sends = ag_start(rp_all, 2 * layers)
@@ -161,6 +154,8 @@
             for cps in (w3_cp, w1_cp, w2_cp):
                 cps[0].start()
         row_tok = lax.broadcasted_iota(jnp.int32, (rows, 1), 0) // heads
+        if l == 0 and hf == 0:
+            len_cp.wait()
         lens = jnp.zeros((rows, 1), jnp.int32)
         for b in range(hb):
             lens = jnp.where(row_tok == b, len_ref[hf * hb + b], lens)
@@ -182,17 +177,23 @@
         xr_v[hf] = resid
         g_all[2 * l + hf, q_me] = rms_norm(resid).astype(BF16)
 
+    def gather_field(e):
+        lane_q = lax.broadcasted_iota(jnp.int32, (top_k, toks), 1) // hb
+        field = jnp.zeros((top_k, toks), F32)
+        for q in range(group):
+            shift = (q - e) * hb % toks
+            tile = rp_all[q]
+            field = jnp.where(lane_q == q, tile if shift == 0 else pltpu.roll(tile, shift, 1), field)
+        return field
+
     def build_masks(l):
         base = me * n_exp + 1
         want = (lax.broadcasted_iota(jnp.int32, (n_exp, toks), 0) + base).astype(F32)
         lane_src = lax.broadcasted_iota(jnp.int32, (group, toks), 1) // hb
         own_src = lane_src == lax.broadcasted_iota(jnp.int32, (group, toks), 0)
         for hf in range(2):
-            code = rp_all[0, hf, l * top_k:(l + 1) * top_k, :]
-            wval = rp_all[0, hf, (layers + l) * top_k:(layers + l + 1) * top_k, :]
-            for j in range(1, group):
-                code = code + rp_all[j, hf, l * top_k:(l + 1) * top_k, :]
-                wval = wval + rp_all[j, hf, (layers + l) * top_k:(layers + l + 1) * top_k, :]
+            code = gather_field(2 * l + hf)
+            wval = gather_field(2 * (layers + l) + hf)
             member = jnp.zeros((n_exp, toks), F32)
             weight = jnp.zeros((n_exp, toks), F32)
             for j in range(top_k):
@@ -299,21 +300,23 @@
                 finish(l - 1, hf)
             attention(l, hf)
             sends += ag_start(g_all.at[2 * l + hf], 2 * l + hf)
-            if l == 0 and hf == 0:
-                wq_cp[1].start()
-                for cp in cache_cp[1]:
-                    cp.start()
         if l == 0:
-            for cp_list in (wo_cp, w3_cp, w1_cp, w2_cp):
-                cp_list[1].start()
             for cp in small[4:]:
                 cp.wait()
             sends += ag_finish(rp_all, 2 * layers)
             build_masks(0)
         sends += ag_finish(g_all.at[2 * l], 2 * l)
+        if l == 0:
+            wq_cp[1].start()
+            for cp in cache_cp[1]:
+                cp.start()
+            wo_cp[1].start()
         first_a = experts(l, 0)
         sends += ag_finish(g_all.at[2 * l + 1], 2 * l + 1)
         later = []
+        if l == 0:
+            for cp_list in (w3_cp, w1_cp, w2_cp):
+                cp_list[1].start()
         first_b = experts(l, 1, lambda: later.extend(second_stage(l, 0, first_a)))
         if l == 0:
             build_masks(1)
@@ -354,8 +357,8 @@
         hb = bat // 2
         toks = group * hb
         slots_n = n_exp * group
-        scratch = [vm(a) for a in args[1:]] + [
-            pltpu.VMEM((group, 2, 2 * layers * top_k, toks), F32),
+        scratch = [pltpu.SMEM(lengths.shape, lengths.dtype)] + [vm(a) for a in args[1:]] + [
+            pltpu.VMEM((group, top_k, toks), F32),
             pltpu.VMEM((layers, 2, slots_n, toks), BF16),
             pltpu.VMEM((layers, 2, 3, toks, slots_n), BF16),
             pltpu.VMEM((phs, group, hb, d_model), BF16),
@@ -372,14 +375,14 @@
             pltpu.VMEM((slots_n, d_model), BF16),
             pltpu.VMEM((slots_n, d_model), BF16),
             pltpu.VMEM((toks, d_model), F32),
-            dma((17,)), dma((layers, bat // 4)),
-            dma((phs + 1, chips)), dma((phs + 1, group)), dma((phs + 1, chips)),
+            dma((18,)), dma((layers, bat // 4)),
+            dma((phs + 1, chips)), dma((phs + 1, chips + 1)),
             dma((phs,)), dma((phs,)), dma((phs, chips)), dma((phs, chips)),
         ]
         return pl.pallas_call(
             functools.partial(step_kernel, chips),
             out_shape=jax.ShapeDtypeStruct(x.shape, x.dtype),
-            in_specs=[pl.BlockSpec(memory_space=pltpu.SMEM)] + [pl.BlockSpec(memory_space=pl.ANY)] * (len(args) - 1),
+            in_specs=[pl.BlockSpec(memory_space=pl.ANY)] * len(args),
             out_specs=pl.BlockSpec(memory_space=pltpu.VMEM),
             scratch_shapes=scratch,
             compiler_params=pltpu.CompilerParams(collective_id=0, has_side_effects=True, vmem_limit_bytes=67043328),

time: 57.7 us -> 55.1 us (0.955)
  Pallas kernels: 56.1 us -> 53.6 us
    pallas_call x1, Pallas kernels: 56.1 us -> 53.6 us  [device_step(): pl.pallas_call(functools.partial(step_kernel, chips), out_shape=jax.Shape...]
where the time goes in v3:
time: 55.1 us; the launch traced here: 55 us
  Pallas kernels  53.6 us (97%)
  local copies, waits for them, and re-layouts  1.32 us (2%)
    pallas_call x1, Pallas kernels, device_step(): pl.pallas_call(functools.partial(step_kernel, chips), out_shape=jax.Shape...  53.6 us
    unnamed x1, local copies, waits for them, and re-layouts  1.32 us

profile of v3, /device:TPU:21, one launch (start us, length us, event | category | flops | bytes accessed | tf_op | source)
XLA Modules:
  0.0 55.0 jit_solution(11608069659886012062)
XLA Ops:
  0.0 53.6 %shard_map.136 = bf16[16,448]{1,0:T(8,128)(2,1)} custom-call(s32[16]{0:T(128)} %len_hbm.1, bf16[16,448]{1,0:T(8,128)(2,1)} %x_hbm.1, bf16[2,16,576,512]{3,2,1,0:T(8,128)(2,1)} %bitcast.8, bf16[2,448,2304]{2,1,0:T(8,128)(2,1)} %wq_hbm.1, bf16[2,448,2048]{2,1,0:T(8,128)(2,1)} %bitcast.10, s32[2,8,16]{2,1,0:T(8,128)} %bitcast.13, s32[2,8,16]{2,1,0:T(8,128)} %bitcast.14, ...), custom_call_target="tpu_custom_call" | custom-call | tf_op jit(solution)/shard_map/pallas_call | solution.py:382
  53.7 1.3 %copy.16 = bf16[16,448]{1,0:T(8,128)(2,1)} copy(bf16[16,448]{1,0:T(8,128)(2,1)} %shard_map.136) | data formatting | bytes 28672

commit v4 on v3

--- a/solution.py
+++ b/solution.py
@@ -130,7 +130,14 @@
     def transpose_wo(l):
         wo_cp[l].wait()
         for k in range(heads * LATENT // 128):
-            wot_v[l, 128 * k:128 * (k + 1), :] = wo_v[l, :, 128 * k:128 * (k + 1)].T
+            wot_v[128 * k:128 * (k + 1), :] = wo_v[l, :, 128 * k:128 * (k + 1)].T
+
+    def transpose_cache(hf):
+        for c in range(2):
+            cache_cp[1][2 * hf + c].wait()
+            for i in range(quad):
+                b = hf * hb + quad * c + i
+                cache_v[0, b, 0:LATENT, :] = cache_v[1, b, 0:LATENT, :].T
 
     def attention(l, hf):
         hidden = rms_norm(xr_v[hf]).astype(BF16)
@@ -142,7 +149,8 @@
             for k in range(q_v.shape[0]):
                 q_v[k, pl.ds(hd, hb, stride=heads), :] = part[:, 128 * k:128 * (k + 1)]
         for c in range(2):
-            cache_cp[l][2 * hf + c].wait()
+            if l == 0:
+                cache_cp[l][2 * hf + c].wait()
             for i in range(quad):
                 b = quad * c + i
                 qb = jnp.concatenate([q_v[k, heads * b:heads * (b + 1), :] for k in range(q_v.shape[0])], axis=1)
@@ -167,12 +175,15 @@
         sc_v[...] = probs
         for b in range(hb):
             pb = sc_v[heads * b:heads * (b + 1), :].astype(BF16)
-            ob = dot_t(pb, cache_v[l, hf * hb + b, 0:LATENT, :])
+            if l == 0:
+                ob = dot_t(pb, cache_v[0, hf * hb + b, 0:LATENT, :])
+            else:
+                ob = dot(pb, cache_v[0, hf * hb + b, 0:LATENT, :])
             for k in range(o_v.shape[0]):
                 o_v[k, heads * b:heads * (b + 1), :] = ob[:, 128 * k:128 * (k + 1)]
         attn = jnp.concatenate([o_v[k, pl.ds(hd, hb, stride=heads), :] for hd in range(heads)
                                 for k in range(o_v.shape[0])], axis=1).astype(BF16)
-        proj = jnp.concatenate([dot(attn, wot_v[l, :, 0:256]), dot(attn, wot_v[l, :, 256:d_model])], axis=1)
+        proj = jnp.concatenate([dot(attn, wot_v[:, 0:256]), dot(attn, wot_v[:, 256:d_model])], axis=1)
         resid = (xr_v[hf] + proj).astype(BF16).astype(F32)
         xr_v[hf] = resid
         g_all[2 * l + hf, q_me] = rms_norm(resid).astype(BF16)
@@ -208,20 +219,14 @@
             rest = owt - hi.astype(F32)
             mid = rest.astype(BF16)
             low = (rest - mid.astype(F32)).astype(BF16)
-            owt_v[l, hf, 0] = hi
-            owt_v[l, hf, 1] = mid
-            owt_v[l, hf, 2] = low
-
-    unroll = 4
+            for k in range(2):
+                for i, term in enumerate((hi, mid, low)):
+                    owt_v[l, hf, k, i * half:(i + 1) * half, :] = term[k * half:(k + 1) * half, :]
 
     def experts(l, hf, between=None):
         ph = 2 * l + hf
         g_in = g_all[ph].reshape(toks, d_model)
         xg_v[...] = dot(oh_v[l, hf], g_in).astype(BF16)
-        gate = dot_t(g_in, w3s_v[l])
-        up = dot_t(g_in, w1s_v[l])
-        shared_h = (jax.nn.silu(gate) * up).astype(BF16)
-        sh_v[...] = dot(shared_h, w2s_v[l])
         if hf == 0:
             for cps in (w3_cp, w1_cp, w2_cp):
                 cps[l].wait()
@@ -244,26 +249,27 @@
             start = pl.multiple_of(pair * 2 * group, 2 * group)
             u_v[pl.ds(start, 2 * group), :] = dot_t(lhs, w2p).astype(BF16)
 
-        def pair_step(i, carry):
-            ready = first_layer(unroll * i)
-            for jj in range(unroll):
-                pair = unroll * i + jj
-                coming = first_layer(pair + 1) if jj < unroll - 1 else None
-                second_layer(pair, ready)
-                ready = coming
-            return carry
-
-        steps = n_exp // (2 * unroll)
-        lax.fori_loop(0, 1, pair_step, 0)
-        if between is not None:
-            between()
-        lax.fori_loop(1, steps, pair_step, 0)
+        def shared_expert():
+            gate = dot_t(g_in, w3s_v[l])
+            up = dot_t(g_in, w1s_v[l])
+            shared_h = (jax.nn.silu(gate) * up).astype(BF16)
+            sh_v[...] = dot(shared_h, w2s_v[l])
+
+        pairs = n_exp // 2
+        ready = first_layer(0)
+        for pair in range(pairs):
+            coming = first_layer(pair + 1) if pair < pairs - 1 else None
+            second_layer(pair, ready)
+            ready = coming
+            if pair == 2:
+                shared_expert()
+            if pair == 3 and between is not None:
+                between()
 
         def part(k):
             sel = pl.ds(pl.multiple_of(k * half, half), half)
-            u_in = u_v[...]
-            return sh_v[sel, :] + (dot(owt_v[l, hf, 0, sel, :], u_in) + dot(owt_v[l, hf, 1, sel, :], u_in)
-                                   + dot(owt_v[l, hf, 2, sel, :], u_in))
+            three = dot(owt_v[l, hf, k], u_v[...])
+            return sh_v[sel, :] + (three[:half] + three[half:2 * half] + three[2 * half:])
 
         p_buf[ph] = part(other).reshape(chips, hb, d_model)
         first = remote(p_buf.at[ph], r1_buf.at[ph], rs1_send.at[ph], rs1_recv.at[ph], partner)
@@ -300,16 +306,18 @@
                 finish(l - 1, hf)
             attention(l, hf)
             sends += ag_start(g_all.at[2 * l + hf], 2 * l + hf)
+            if l == 0 and hf == 0:
+                for cp in cache_cp[1]:
+                    cp.start()
         if l == 0:
             for cp in small[4:]:
                 cp.wait()
             sends += ag_finish(rp_all, 2 * layers)
             build_masks(0)
+            transpose_cache(0)
         sends += ag_finish(g_all.at[2 * l], 2 * l)
         if l == 0:
             wq_cp[1].start()
-            for cp in cache_cp[1]:
-                cp.start()
             wo_cp[1].start()
         first_a = experts(l, 0)
         sends += ag_finish(g_all.at[2 * l + 1], 2 * l + 1)
@@ -317,11 +325,16 @@
         if l == 0:
             for cp_list in (w3_cp, w1_cp, w2_cp):
                 cp_list[1].start()
-        first_b = experts(l, 1, lambda: later.extend(second_stage(l, 0, first_a)))
         if l == 0:
+            later += second_stage(l, 0, first_a)
+            first_b = experts(l, 1)
             build_masks(1)
             transpose_wo(1)
+        else:
+            first_b = experts(l, 1, lambda: later.extend(second_stage(l, 0, first_a)))
         sends += later + second_stage(l, 1, first_b)
+        if l == 0:
+            transpose_cache(1)
     for hf in range(2):
         finish(layers - 1, hf)
     for cp in sends:
@@ -360,7 +373,7 @@
         scratch = [pltpu.SMEM(lengths.shape, lengths.dtype)] + [vm(a) for a in args[1:]] + [
             pltpu.VMEM((group, top_k, toks), F32),
             pltpu.VMEM((layers, 2, slots_n, toks), BF16),
-            pltpu.VMEM((layers, 2, 3, toks, slots_n), BF16),
+            pltpu.VMEM((layers, 2, 2, 3 * toks // 2, slots_n), BF16),
             pltpu.VMEM((phs, group, hb, d_model), BF16),
             pltpu.VMEM((phs, chips, hb, d_model), F32),
             pltpu.VMEM((phs, chips, hb, d_model), F32),
@@ -368,7 +381,7 @@
             pltpu.VMEM((phs, chips, hb, d_model), F32),
             pltpu.VMEM((phs, chips, hb, d_model), F32),
             pltpu.VMEM((2, hb, d_model), F32),
-            pltpu.VMEM((layers, heads * LATENT, d_model), BF16),
+            pltpu.VMEM((heads * LATENT, d_model), BF16),
             pltpu.VMEM((-(-kv_dim // 128), heads * hb, 128), F32),
             pltpu.VMEM((heads * hb, seq_len), F32),
             pltpu.VMEM((LATENT // 128, heads * hb, 128), F32),
@@ -382,10 +395,10 @@
         return pl.pallas_call(
             functools.partial(step_kernel, chips),
             out_shape=jax.ShapeDtypeStruct(x.shape, x.dtype),
-            in_specs=[pl.BlockSpec(memory_space=pl.ANY)] * len(args),
+            in_specs=[pl.BlockSpec(memory_space=pltpu.HBM)] * len(args),
             out_specs=pl.BlockSpec(memory_space=pltpu.VMEM),
             scratch_shapes=scratch,
-            compiler_params=pltpu.CompilerParams(collective_id=0, has_side_effects=True, vmem_limit_bytes=67043328),
-        )(*args)
+            compiler_params=pltpu.CompilerParams(collective_id=0, has_side_effects=True, vmem_limit_bytes=56000000),
+        )(*[pltpu.with_memory_space_constraint(a, pltpu.HBM) for a in args])
 
     return jax.shard_map(device_step, mesh=mesh, in_specs=in_specs, out_specs=P(tok_axes, None), check_vma=False)

time: 55.1 us -> 52.1 us (0.946)
  Pallas kernels: 53.6 us -> 51.5 us
  local copies, waits for them, and re-layouts: 1.32 us -> 0.61 us
    pallas_call x1, Pallas kernels: 53.6 us -> 51.5 us  [device_step(): pl.pallas_call(functools.partial(step_kernel, chips), out_shape=jax.Shape...]
    unnamed x1, local copies, waits for them, and re-layouts: 1.32 us -> 0.61 us
where the time goes in v4:
time: 52.1 us
  Pallas kernels  51.5 us (99%)
  local copies, waits for them, and re-layouts  0.61 us (1%)
    pallas_call x1, Pallas kernels, device_step(): pl.pallas_call(functools.partial(step_kernel, chips), out_shape=jax.Shape...  51.5 us

profile of v4, /device:TPU:21, one launch (start us, length us, event | category | flops | bytes accessed | tf_op | source)
XLA Modules:
  0.0 52.1 jit_solution(12715963658089581167)
XLA Ops:
  0.0 51.5 %shard_map.136 = bf16[16,448]{1,0:T(8,128)(2,1)S(1)} custom-call(s32[16]{0:T(128)} %len_hbm.1, bf16[16,448]{1,0:T(8,128)(2,1)} %x_hbm.1, bf16[2,16,576,512]{3,2,1,0:T(8,128)(2,1)} %bitcast.8, bf16[2,448,2304]{2,1,0:T(8,128)(2,1)} %wq_hbm.1, bf16[2,448,2048]{2,1,0:T(8,128)(2,1)} %bitcast.10, s32[2,8,16]{2,1,0:T(8,128)} %bitcast.13, s32[2,8,16]{2,1,0:T(8,128)} %bitcast.14, ...), custom_call_target="tpu_custom_call" | custom-call | tf_op jit(solution)/shard_map/pallas_call | solution.py:395
  51.5 0.6 %copy.16 = bf16[16,448]{1,0:T(8,128)(2,1)} copy(bf16[16,448]{1,0:T(8,128)(2,1)S(1)} %shard_map.136) | data formatting | bytes 28672

commit v5 on v4

--- a/solution.py
+++ b/solution.py
@@ -31,8 +31,8 @@
                 w1s_hbm, w3s_hbm, w2s_hbm, out_ref,
                 len_ref, x_v, cache_v, wq_v, wo_v, ids_v, slots_v, rw_v, w1_v, w3_v, w2_v, w1s_v, w3s_v, w2s_v,
                 rp_all, oh_v, owt_v, g_all, p_buf, own_buf, r1_buf, s_buf, r2_buf,
-                xr_v, wot_v, q_v, sc_v, o_v, xg_v, u_v, sh_v,
-                loc_sem, cache_sem, ag_send, ag_recv, rs1_send, rs1_recv, rs2_send, rs2_recv):
+                xr_v, wot_v, w2t_v, q_v, sc_v, o_v, xg_v, u_v, sh_v,
+                loc_sem, cache_sem, ag_send, ag_recv, rs1_send, rs1_recv, rs2_send, rs2_recv, wq_sem):
     layers, bat, kv_dim, seq_len = cache_v.shape
     d_model = x_v.shape[1]
     heads = wq_v.shape[2] // kv_dim
@@ -64,7 +64,10 @@
 
     small = [load(x_hbm, x_v, 0), load(ids_hbm, ids_v, 1), load(slots_hbm, slots_v, 2), load(rw_hbm, rw_v, 3),
              load(w1s_hbm, w1s_v, 4), load(w3s_hbm, w3s_v, 5), load(w2s_hbm, w2s_v, 6)]
-    wq_cp = [load(wq_hbm.at[l], wq_v.at[l], 7 + l) for l in range(layers)]
+    q_cols = wq_v.shape[2]
+    q_part = q_cols // 3
+    wq_cp = [[pltpu.make_async_copy(wq_hbm.at[l, :, pl.ds(q_part * c, q_part)], wq_v.at[l, :, pl.ds(q_part * c, q_part)],
+                                    wq_sem.at[l, c]) for c in range(3)] for l in range(layers)]
     wo_cp = [load(wo_hbm.at[l], wo_v.at[l], 9 + l) for l in range(layers)]
     w3_cp = [load(w3_hbm.at[l], w3_v.at[l], 11 + l) for l in range(layers)]
     w1_cp = [load(w1_hbm.at[l], w1_v.at[l], 13 + l) for l in range(layers)]
@@ -73,15 +76,17 @@
                                        cache_sem.at[l, c]) for c in range(bat // quad)] for l in range(layers)]
 
     small[0].start()
-    wq_cp[0].start()
+    for cp in wq_cp[0]:
+        cp.start()
     len_cp = pltpu.make_async_copy(len_hbm, len_ref, loc_sem.at[17])
     for cp in small[1:4]:
         cp.start()
-    cache_cp[0][0].start()
+    len_cp.start()
+    for cp in cache_cp[0][:2]:
+        cp.start()
     wo_cp[0].start()
-    for cp in cache_cp[0][1:]:
-        cp.start()
-    len_cp.start()
+    for cp in cache_cp[0][2:]:
+        cp.start()
     for cp in small[4:]:
         cp.start()
 
@@ -132,58 +137,75 @@
         for k in range(heads * LATENT // 128):
             wot_v[128 * k:128 * (k + 1), :] = wo_v[l, :, 128 * k:128 * (k + 1)].T
 
-    def transpose_cache(hf):
-        for c in range(2):
-            cache_cp[1][2 * hf + c].wait()
-            for i in range(quad):
-                b = hf * hb + quad * c + i
-                cache_v[0, b, 0:LATENT, :] = cache_v[1, b, 0:LATENT, :].T
+    def transpose_w2(l):
+        w2_cp[l].wait()
+        for n in range(n_exp):
+            w2t_v[ff * n:ff * (n + 1), :] = w2_v[l, n].T
+
+    def transpose_cache(c):
+        cache_cp[1][c].wait()
+        for b in range(quad * c, quad * (c + 1)):
+            cache_v[0, b, 0:LATENT, :] = cache_v[1, b, 0:LATENT, :].T
 
     def attention(l, hf):
-        hidden = rms_norm(xr_v[hf]).astype(BF16)
-        if hf == 0:
-            wq_cp[l].wait()
-        q = dot(hidden, wq_v[l])
-        for hd in range(heads):
-            part = q if hd == 0 else pltpu.roll(q, heads * kv_dim - hd * kv_dim, 1)
-            for k in range(q_v.shape[0]):
-                q_v[k, pl.ds(hd, hb, stride=heads), :] = part[:, 128 * k:128 * (k + 1)]
-        for c in range(2):
+        halves = (0, 1) if l == 0 else (hf,)
+        if l > 0 or hf == 0:
+            x_in = xr_v[...].reshape(bat, d_model) if l == 0 else xr_v[hf]
+            hidden = rms_norm(x_in).astype(BF16)
+            q = []
+            if l > 0 and hf == 0:
+                for cp in wq_cp[l]:
+                    cp.wait()
+            for c in range(3):
+                if l == 0:
+                    wq_cp[l][c].wait()
+                q.append(dot(hidden, wq_v[l, :, q_part * c:q_part * (c + 1)]))
+            q = jnp.concatenate(q, axis=1)
+            for hd in range(heads):
+                part = q if hd == 0 else pltpu.roll(q, q_cols - hd * kv_dim, 1)
+                for i, h in enumerate(halves):
+                    for k in range(q_v.shape[1]):
+                        q_v[h, k, pl.ds(hd, hb, stride=heads), :] = part[hb * i:hb * (i + 1), 128 * k:128 * (k + 1)]
+        if l == 0 and hf == 0:
+            len_cp.wait()
+        for grp in (((0,), (1,)) if l == 0 and hf == 0 else ((0, 1),)):
+            first, count = heads * quad * grp[0], heads * quad * len(grp)
+            seqs = range(quad * grp[0], quad * (grp[-1] + 1))
             if l == 0:
-                cache_cp[l][2 * hf + c].wait()
-            for i in range(quad):
-                b = quad * c + i
-                qb = jnp.concatenate([q_v[k, heads * b:heads * (b + 1), :] for k in range(q_v.shape[0])], axis=1)
+                for c in grp:
+                    cache_cp[l][2 * hf + c].wait()
+            for b in seqs:
+                qb = jnp.concatenate([q_v[hf, k, heads * b:heads * (b + 1), :] for k in range(q_v.shape[1])], axis=1)
                 qb = qb[:, :kv_dim].astype(BF16)
                 sc_v[heads * b:heads * (b + 1), :] = dot(qb, cache_v[l, hf * hb + b])
-            if l == 0 and hf == 0 and c == 0:
-                transpose_wo(0)
-        if l == 0 and hf == 0:
-            for cps in (w3_cp, w1_cp, w2_cp):
-                cps[0].start()
-        row_tok = lax.broadcasted_iota(jnp.int32, (rows, 1), 0) // heads
-        if l == 0 and hf == 0:
-            len_cp.wait()
-        lens = jnp.zeros((rows, 1), jnp.int32)
-        for b in range(hb):
-            lens = jnp.where(row_tok == b, len_ref[hf * hb + b], lens)
-        valid = lax.broadcasted_iota(jnp.int32, (rows, seq_len), 1) < lens
-        scores = jnp.where(valid, sc_v[...] * ATT_SCALE, -jnp.inf)
-        top = jnp.max(scores, axis=1, keepdims=True)
-        ex = jnp.exp(scores - top)
-        probs = ex / jnp.sum(ex, axis=1, keepdims=True)
-        sc_v[...] = probs
-        for b in range(hb):
-            pb = sc_v[heads * b:heads * (b + 1), :].astype(BF16)
-            if l == 0:
-                ob = dot_t(pb, cache_v[0, hf * hb + b, 0:LATENT, :])
-            else:
-                ob = dot(pb, cache_v[0, hf * hb + b, 0:LATENT, :])
-            for k in range(o_v.shape[0]):
-                o_v[k, heads * b:heads * (b + 1), :] = ob[:, 128 * k:128 * (k + 1)]
+            row_tok = (lax.broadcasted_iota(jnp.int32, (count, 1), 0) + first) // heads
+            lens = jnp.zeros((count, 1), jnp.int32)
+            for b in seqs:
+                lens = jnp.where(row_tok == b, len_ref[hf * hb + b], lens)
+            valid = lax.broadcasted_iota(jnp.int32, (count, seq_len), 1) < lens
+            scores = jnp.where(valid, sc_v[first:first + count, :] * ATT_SCALE, -jnp.inf)
+            top = jnp.max(scores, axis=1, keepdims=True)
+            ex = jnp.exp(scores - top)
+            sc_v[first:first + count, :] = ex / jnp.sum(ex, axis=1, keepdims=True)
+            for b in seqs:
+                pb = sc_v[heads * b:heads * (b + 1), :].astype(BF16)
+                if l == 0:
+                    ob = dot_t(pb, cache_v[0, hf * hb + b, 0:LATENT, :])
+                else:
+                    ob = dot(pb, cache_v[0, hf * hb + b, 0:LATENT, :])
+                for k in range(o_v.shape[0]):
+                    o_v[k, heads * b:heads * (b + 1), :] = ob[:, 128 * k:128 * (k + 1)]
+            if l == 0 and hf == 0 and grp[0] == 0:
+                for cps in (w2_cp, w3_cp, w1_cp):
+                    cps[0].start()
         attn = jnp.concatenate([o_v[k, pl.ds(hd, hb, stride=heads), :] for hd in range(heads)
                                 for k in range(o_v.shape[0])], axis=1).astype(BF16)
-        proj = jnp.concatenate([dot(attn, wot_v[:, 0:256]), dot(attn, wot_v[:, 256:d_model])], axis=1)
+        if l == 0:
+            if hf == 0:
+                wo_cp[0].wait()
+            proj = jnp.concatenate([dot_t(attn, wo_v[0, 0:256]), dot_t(attn, wo_v[0, 256:d_model])], axis=1)
+        else:
+            proj = jnp.concatenate([dot(attn, wot_v[:, 0:256]), dot(attn, wot_v[:, 256:d_model])], axis=1)
         resid = (xr_v[hf] + proj).astype(BF16).astype(F32)
         xr_v[hf] = resid
         g_all[2 * l + hf, q_me] = rms_norm(resid).astype(BF16)
@@ -228,15 +250,14 @@
         g_in = g_all[ph].reshape(toks, d_model)
         xg_v[...] = dot(oh_v[l, hf], g_in).astype(BF16)
         if hf == 0:
-            for cps in (w3_cp, w1_cp, w2_cp):
+            for cps in (w3_cp, w1_cp):
                 cps[l].wait()
 
         def first_layer(pair):
             hid = []
             for e in range(2):
                 n = 2 * pair + e
-                start = pl.multiple_of(n * group, group)
-                xin = xg_v[pl.ds(start, group), :]
+                xin = xg_v[group * n:group * (n + 1), :]
                 w31 = jnp.concatenate([w3_v[l, n], w1_v[l, n]], axis=1)
                 both = dot(xin, w31)
                 hid.append((jax.nn.silu(both[:, :ff]) * both[:, ff:]).astype(BF16))
@@ -245,9 +266,7 @@
                                     jnp.concatenate([zero, hid[1]], axis=1)], axis=0)
 
         def second_layer(pair, lhs):
-            w2p = jnp.concatenate([w2_v[l, 2 * pair], w2_v[l, 2 * pair + 1]], axis=1)
-            start = pl.multiple_of(pair * 2 * group, 2 * group)
-            u_v[pl.ds(start, 2 * group), :] = dot_t(lhs, w2p).astype(BF16)
+            u_v[2 * group * pair:2 * group * (pair + 1), :] = dot(lhs, w2t_v[2 * ff * pair:2 * ff * (pair + 1), :]).astype(BF16)
 
         def shared_expert():
             gate = dot_t(g_in, w3s_v[l])
@@ -300,41 +319,44 @@
             tot = tot + r2_buf[ph, j]
         xr_v[hf] = (xr_v[hf] + tot).astype(BF16).astype(F32)
 
-    for l in range(layers):
-        for hf in range(2):
-            if l > 0:
-                finish(l - 1, hf)
-            attention(l, hf)
-            sends += ag_start(g_all.at[2 * l + hf], 2 * l + hf)
-            if l == 0 and hf == 0:
-                for cp in cache_cp[1]:
-                    cp.start()
-        if l == 0:
-            for cp in small[4:]:
-                cp.wait()
-            sends += ag_finish(rp_all, 2 * layers)
-            build_masks(0)
-            transpose_cache(0)
-        sends += ag_finish(g_all.at[2 * l], 2 * l)
-        if l == 0:
-            wq_cp[1].start()
-            wo_cp[1].start()
-        first_a = experts(l, 0)
-        sends += ag_finish(g_all.at[2 * l + 1], 2 * l + 1)
-        later = []
-        if l == 0:
-            for cp_list in (w3_cp, w1_cp, w2_cp):
-                cp_list[1].start()
-        if l == 0:
-            later += second_stage(l, 0, first_a)
-            first_b = experts(l, 1)
-            build_masks(1)
-            transpose_wo(1)
-        else:
-            first_b = experts(l, 1, lambda: later.extend(second_stage(l, 0, first_a)))
-        sends += later + second_stage(l, 1, first_b)
-        if l == 0:
-            transpose_cache(1)
+    attention(0, 0)
+    sends += ag_start(g_all.at[0], 0)
+    attention(0, 1)
+    sends += ag_start(g_all.at[1], 1)
+    for cp in cache_cp[1]:
+        cp.start()
+    for cp in small[4:]:
+        cp.wait()
+    sends += ag_finish(rp_all, 2 * layers)
+    build_masks(0)
+    transpose_w2(0)
+    sends += ag_finish(g_all.at[0], 0)
+    for cp in wq_cp[1] + [wo_cp[1]]:
+        cp.start()
+    later = []
+    first_a = experts(0, 0)
+    sends += ag_finish(g_all.at[1], 1)
+    for cp_list in (w3_cp, w1_cp, w2_cp):
+        cp_list[1].start()
+    first_b = experts(0, 1, lambda: later.extend(second_stage(0, 0, first_a)))
+    build_masks(1)
+    transpose_cache(0)
+    later += second_stage(0, 1, first_b)
+    for c in range(1, bat // quad):
+        transpose_cache(c)
+    transpose_wo(1)
+    finish(0, 0)
+    attention(1, 0)
+    sends += ag_start(g_all.at[2], 2)
+    finish(0, 1)
+    attention(1, 1)
+    sends += ag_start(g_all.at[3], 3)
+    transpose_w2(1)
+    sends += ag_finish(g_all.at[2], 2)
+    first_a = experts(1, 0)
+    sends += ag_finish(g_all.at[3], 3)
+    first_b = experts(1, 1, lambda: later.extend(second_stage(1, 0, first_a)))
+    sends += later + second_stage(1, 1, first_b)
     for hf in range(2):
         finish(layers - 1, hf)
     for cp in sends:
@@ -382,7 +404,8 @@
             pltpu.VMEM((phs, chips, hb, d_model), F32),
             pltpu.VMEM((2, hb, d_model), F32),
             pltpu.VMEM((heads * LATENT, d_model), BF16),
-            pltpu.VMEM((-(-kv_dim // 128), heads * hb, 128), F32),
+            pltpu.VMEM((n_exp * ff, d_model), BF16),
+            pltpu.VMEM((2, -(-kv_dim // 128), heads * hb, 128), F32),
             pltpu.VMEM((heads * hb, seq_len), F32),
             pltpu.VMEM((LATENT // 128, heads * hb, 128), F32),
             pltpu.VMEM((slots_n, d_model), BF16),
@@ -390,7 +413,7 @@
             pltpu.VMEM((toks, d_model), F32),
             dma((18,)), dma((layers, bat // 4)),
             dma((phs + 1, chips)), dma((phs + 1, chips + 1)),
-            dma((phs,)), dma((phs,)), dma((phs, chips)), dma((phs, chips)),
+            dma((phs,)), dma((phs,)), dma((phs, chips)), dma((phs, chips)), dma((layers, 3)),
         ]
         return pl.pallas_call(
             functools.partial(step_kernel, chips),

time: 52.1 us -> 52 us (level)
  no operation moved by 1% of the time
where the time goes in v5:
time: 52 us
  Pallas kernels  51.4 us (99%)
  local copies, waits for them, and re-layouts  0.61 us (1%)
    pallas_call x1, Pallas kernels, device_step(): pl.pallas_call(functools.partial(step_kernel, chips), out_shape=jax.Shape...  51.4 us

profile of v5, /device:TPU:21, one launch (start us, length us, event | category | flops | bytes accessed | tf_op | source)
XLA Modules:
  0.0 52.0 jit_solution(9580782983443123080)
XLA Ops:
  0.0 51.4 %shard_map.136 = bf16[16,448]{1,0:T(8,128)(2,1)S(1)} custom-call(s32[16]{0:T(128)} %len_hbm.1, bf16[16,448]{1,0:T(8,128)(2,1)} %x_hbm.1, bf16[2,16,576,512]{3,2,1,0:T(8,128)(2,1)} %bitcast.8, bf16[2,448,2304]{2,1,0:T(8,128)(2,1)} %wq_hbm.1, bf16[2,448,2048]{2,1,0:T(8,128)(2,1)} %bitcast.10, s32[2,8,16]{2,1,0:T(8,128)} %bitcast.13, s32[2,8,16]{2,1,0:T(8,128)} %bitcast.14, ...), custom_call_target="tpu_custom_call" | custom-call | tf_op jit(solution)/shard_map/pallas_call | solution.py:418
  51.4 0.6 %copy.16 = bf16[16,448]{1,0:T(8,128)(2,1)} copy(bf16[16,448]{1,0:T(8,128)(2,1)S(1)} %shard_map.136) | data formatting | bytes 28672

commit v6 on v5

--- a/solution.py
+++ b/solution.py
@@ -30,7 +30,7 @@
 def step_kernel(chips, len_hbm, x_hbm, cache_hbm, wq_hbm, wo_hbm, ids_hbm, slots_hbm, rw_hbm, w1_hbm, w3_hbm, w2_hbm,
                 w1s_hbm, w3s_hbm, w2s_hbm, out_ref,
                 len_ref, x_v, cache_v, wq_v, wo_v, ids_v, slots_v, rw_v, w1_v, w3_v, w2_v, w1s_v, w3s_v, w2s_v,
-                rp_all, oh_v, owt_v, g_all, p_buf, own_buf, r1_buf, s_buf, r2_buf,
+                rp_all, oh_v, owt_v, g_all, p_buf, own_buf, r1_buf, s_buf, r2_buf, t_buf, a_buf,
                 xr_v, wot_v, w2t_v, q_v, sc_v, o_v, xg_v, u_v, sh_v,
                 loc_sem, cache_sem, ag_send, ag_recv, rs1_send, rs1_recv, rs2_send, rs2_recv, wq_sem):
     layers, bat, kv_dim, seq_len = cache_v.shape
@@ -282,7 +282,7 @@
             ready = coming
             if pair == 2:
                 shared_expert()
-            if pair == 3 and between is not None:
+            if pair == 2 and between is not None:
                 between()
 
         def part(k):
@@ -301,22 +301,36 @@
         first.wait_recv()
         s_buf[ph] = own_buf[ph] + r1_buf[ph]
         cps = [first]
-        for i, delta in enumerate(far_first):
-            dst = chip_at(delta)
-            cp = remote(s_buf.at[ph, dst], r2_buf.at[ph, chip], rs2_send.at[ph, i], rs2_recv.at[ph, chip], 2 * dst + core)
-            cp.start()
-            cps.append(cp)
-        r2_buf[ph, chip] = s_buf[ph, chip]
+        hops = ((4, 2, t_buf.at[ph, 0], 4), (3, 1, t_buf.at[ph, 1], 5), (chips - 3, chips - 1, t_buf.at[ph, 2], 6),
+                (1, 1, r2_buf.at[ph, 0], 0), (chips - 1, chips - 1, r2_buf.at[ph, 1], 1))
+        for i, (owner, to, dst, sem) in enumerate(hops):
+            cps.append(remote(s_buf.at[ph, chip_at(owner)], dst, rs2_send.at[ph, i], rs2_recv.at[ph, sem],
+                              2 * chip_at(to) + core))
+            cps[-1].start()
+        return cps
+
+    def arrived(dst, ph, sem):
+        remote(dst, dst, rs2_send.at[ph, 0], rs2_recv.at[ph, sem], partner).wait_recv()
+
+    def third_stage(l, hf):
+        ph = 2 * l + hf
+        for i in range(3):
+            arrived(t_buf.at[ph, i], ph, 4 + i)
+        ahead, behind = chip_at(2), chip_at(chips - 2)
+        a_buf[ph, 0] = s_buf[ph, ahead] + (t_buf[ph, 0] + t_buf[ph, 1])
+        cps = [remote(a_buf.at[ph, 0], r2_buf.at[ph, 2], rs2_send.at[ph, 5], rs2_recv.at[ph, 2], 2 * ahead + core)]
+        cps[0].start()
+        a_buf[ph, 1] = s_buf[ph, behind] + t_buf[ph, 2]
+        cps.append(remote(a_buf.at[ph, 1], r2_buf.at[ph, 3], rs2_send.at[ph, 6], rs2_recv.at[ph, 3], 2 * behind + core))
+        cps[1].start()
         return cps
 
     def finish(l, hf):
         ph = 2 * l + hf
-        for i, delta in enumerate(near_first):
-            src = chip_at(chips - delta)
-            remote(s_buf.at[ph, src], r2_buf.at[ph, src], rs2_send.at[ph, 0], rs2_recv.at[ph, src], partner).wait_recv()
-        tot = r2_buf[ph, 0]
-        for j in range(1, chips):
-            tot = tot + r2_buf[ph, j]
+        tot = s_buf[ph, chip]
+        for i in range(4):
+            arrived(r2_buf.at[ph, i], ph, i)
+            tot = tot + r2_buf[ph, i]
         xr_v[hf] = (xr_v[hf] + tot).astype(BF16).astype(F32)
 
     attention(0, 0)
@@ -342,9 +356,11 @@
     build_masks(1)
     transpose_cache(0)
     later += second_stage(0, 1, first_b)
+    later += third_stage(0, 0)
     for c in range(1, bat // quad):
         transpose_cache(c)
     transpose_wo(1)
+    later += third_stage(0, 1)
     finish(0, 0)
     attention(1, 0)
     sends += ag_start(g_all.at[2], 2)
@@ -356,7 +372,8 @@
     first_a = experts(1, 0)
     sends += ag_finish(g_all.at[3], 3)
     first_b = experts(1, 1, lambda: later.extend(second_stage(1, 0, first_a)))
-    sends += later + second_stage(1, 1, first_b)
+    sends += later + third_stage(1, 0) + second_stage(1, 1, first_b)
+    sends += third_stage(1, 1)
     for hf in range(2):
         finish(layers - 1, hf)
     for cp in sends:
@@ -401,7 +418,9 @@
             pltpu.VMEM((phs, chips, hb, d_model), F32),
             pltpu.VMEM((phs, chips, hb, d_model), F32),
             pltpu.VMEM((phs, chips, hb, d_model), F32),
-            pltpu.VMEM((phs, chips, hb, d_model), F32),
+            pltpu.VMEM((phs, 4, hb, d_model), F32),
+            pltpu.VMEM((phs, 3, hb, d_model), F32),
+            pltpu.VMEM((phs, 2, hb, d_model), F32),
             pltpu.VMEM((2, hb, d_model), F32),
             pltpu.VMEM((heads * LATENT, d_model), BF16),
             pltpu.VMEM((n_exp * ff, d_model), BF16),

time: 52 us -> 57.2 us (1.10)
  the two profiles are of different devices: /device:TPU:21 before, /device:TPU:22 now
where the time goes in v6:
time: 57.2 us; the launch traced here: 57.1 us
  Pallas kernels  56.5 us (99%)
  local copies, waits for them, and re-layouts  0.61 us (1%)
    pallas_call x1, Pallas kernels, device_step(): pl.pallas_call(functools.partial(step_kernel, chips), out_shape=jax.Shape...  56.5 us

profile of v6, /device:TPU:22, one launch (start us, length us, event | category | flops | bytes accessed | tf_op | source)
XLA Modules:
  0.0 57.1 jit_solution(17479907248957864346)
XLA Ops:
  0.0 56.5 %shard_map.136 = bf16[16,448]{1,0:T(8,128)(2,1)S(1)} custom-call(s32[16]{0:T(128)} %len_hbm.1, bf16[16,448]{1,0:T(8,128)(2,1)} %x_hbm.1, bf16[2,16,576,512]{3,2,1,0:T(8,128)(2,1)} %bitcast.8, bf16[2,448,2304]{2,1,0:T(8,128)(2,1)} %wq_hbm.1, bf16[2,448,2048]{2,1,0:T(8,128)(2,1)} %bitcast.10, s32[2,8,16]{2,1,0:T(8,128)} %bitcast.13, s32[2,8,16]{2,1,0:T(8,128)} %bitcast.14, ...), custom_call_target="tpu_custom_call" | custom-call | tf_op jit(solution)/shard_map/pallas_call | solution.py:437
  56.5 0.6 %copy.16 = bf16[16,448]{1,0:T(8,128)(2,1)} copy(bf16[16,448]{1,0:T(8,128)(2,1)S(1)} %shard_map.136) | data formatting | bytes 28672

commit v7 on v5

--- a/solution.py
+++ b/solution.py
@@ -107,17 +107,24 @@
             cp.start()
         return cps
 
-    def ag_finish(buf, ph):
+    def ag_forward(buf, ph):
         for i, delta in enumerate(near_first):
             src = chip_at(chips - delta)
             q = core * chips + src
             remote(buf.at[q], buf.at[q], ag_send.at[ph, 0], ag_recv.at[ph, src], partner).wait_recv()
         mine = buf.at[pl.ds(core * chips, chips)]
+        cp = remote(mine, mine, ag_send.at[ph, chips - 1], ag_recv.at[ph, chips], partner)
+        cp.start()
+        return [cp]
+
+    def ag_wait(buf, ph):
         theirs = buf.at[pl.ds(other * chips, chips)]
-        cp = remote(mine, mine, ag_send.at[ph, chips - 1], ag_recv.at[ph, chips], partner)
-        cp.start()
         remote(theirs, theirs, ag_send.at[ph, chips - 1], ag_recv.at[ph, chips], partner).wait_recv()
-        return [cp]
+
+    def ag_finish(buf, ph):
+        cps = ag_forward(buf, ph)
+        ag_wait(buf, ph)
+        return cps
 
     for cp in small[1:4]:
         cp.wait()
@@ -282,7 +289,7 @@
             ready = coming
             if pair == 2:
                 shared_expert()
-            if pair == 3 and between is not None:
+            if pair == 2 and between is not None:
                 between()
 
         def part(k):
@@ -329,16 +336,19 @@
         cp.wait()
     sends += ag_finish(rp_all, 2 * layers)
     build_masks(0)
+    sends += ag_forward(g_all.at[0], 0)
     transpose_w2(0)
-    sends += ag_finish(g_all.at[0], 0)
+    ag_wait(g_all.at[0], 0)
     for cp in wq_cp[1] + [wo_cp[1]]:
         cp.start()
     later = []
     first_a = experts(0, 0)
-    sends += ag_finish(g_all.at[1], 1)
+    sends += ag_forward(g_all.at[1], 1)
     for cp_list in (w3_cp, w1_cp, w2_cp):
         cp_list[1].start()
-    first_b = experts(0, 1, lambda: later.extend(second_stage(0, 0, first_a)))
+    later += second_stage(0, 0, first_a)
+    ag_wait(g_all.at[1], 1)
+    first_b = experts(0, 1)
     build_masks(1)
     transpose_cache(0)
     later += second_stage(0, 1, first_b)

time: 52 us -> 51.3 us (0.987)
  Pallas kernels: 51.4 us -> 50.6 us
    pallas_call x1, Pallas kernels: 51.4 us -> 50.6 us  [device_step(): pl.pallas_call(functools.partial(step_kernel, chips), out_shape=jax.Shape...]
where the time goes in v7:
time: 51.3 us; the launch traced here: 51.2 us
  Pallas kernels  50.6 us (99%)
  local copies, waits for them, and re-layouts  0.61 us (1%)
    pallas_call x1, Pallas kernels, device_step(): pl.pallas_call(functools.partial(step_kernel, chips), out_shape=jax.Shape...  50.6 us

profile of v7, /device:TPU:21, one launch (start us, length us, event | category | flops | bytes accessed | tf_op | source)
XLA Modules:
  0.0 51.2 jit_solution(13005028449281313503)
XLA Ops:
  0.0 50.6 %shard_map.136 = bf16[16,448]{1,0:T(8,128)(2,1)S(1)} custom-call(s32[16]{0:T(128)} %len_hbm.1, bf16[16,448]{1,0:T(8,128)(2,1)} %x_hbm.1, bf16[2,16,576,512]{3,2,1,0:T(8,128)(2,1)} %bitcast.8, bf16[2,448,2304]{2,1,0:T(8,128)(2,1)} %wq_hbm.1, bf16[2,448,2048]{2,1,0:T(8,128)(2,1)} %bitcast.10, s32[2,8,16]{2,1,0:T(8,128)} %bitcast.13, s32[2,8,16]{2,1,0:T(8,128)} %bitcast.14, ...), custom_call_target="tpu_custom_call" | custom-call | tf_op jit(solution)/shard_map/pallas_call | solution.py:428
  50.6 0.6 %copy.16 = bf16[16,448]{1,0:T(8,128)(2,1)} copy(bf16[16,448]{1,0:T(8,128)(2,1)S(1)} %shard_map.136) | data formatting | bytes 28672
